TPU v7x, 256 devices: a whole 4x4x8 slice. The times are simulated.
256 devices in a mesh: grp: 16 (over y_lo, z), mem: 16 (over y_hi, x, core).
Axes of the slice: x: 4, y: 4 (y_hi: 2, y_lo: 2; y = y_hi * 2 + y_lo), z: 8, core: 2. Of those that a mesh axis runs over, the one named last changes fastest.
Arguments:
- client_input: bfloat16 [16, 16, 128, 896], P('grp', 'mem'), may hold values from -6 to 6
- client_gain: float32 [16, 896], P('mem'), may hold values from 0.5 to 1.5
- w_query: bfloat16 [16, 896, 896], P('mem'), may hold values from -1.5 to 1.5
- w_keyval: bfloat16 [16, 896, 256], P('mem'), may hold values from -0.5 to 0.5
- w_out: bfloat16 [16, 896, 896], P('mem'), may hold values from -0.1875 to 0.1875
- server_gain: float32 [16, 896], P('grp'), may hold values from 0.5 to 1.5
- w_gate: bfloat16 [16, 896, 4864], P('grp', None, 'mem'), may hold values from -0.1875 to 0.1875
- w_up: bfloat16 [16, 896, 4864], P('grp', None, 'mem'), may hold values from -0.1875 to 0.1875
- w_down: bfloat16 [16, 4864, 896], P('grp', 'mem'), may hold values from -0.078125 to 0.078125
- out_grad: bfloat16 [16, 16, 128, 896], P('grp', 'mem'), may hold values from -6 to 6
- valid: int32 [16, 16], P('grp', 'mem'), may hold values from 64 to 128
Outputs:
- server_out: bfloat16 [16, 16, 128, 896], P('grp', 'mem')
- grad_query: bfloat16 [16, 896, 896], P('mem')
- grad_keyval: bfloat16 [16, 896, 256], P('mem')
- grad_out: bfloat16 [16, 896, 896], P('mem')
- grad_gate: bfloat16 [16, 896, 4864], P('grp', None, 'mem')
- grad_up: bfloat16 [16, 896, 4864], P('grp', None, 'mem')
- grad_down: bfloat16 [16, 4864, 896], P('grp', 'mem')
All inputs are finite; a program needn't handle non-finite values.
Results may differ from a plain program's by a relative error of at most 0.03.
Values may be sent and summed in bfloat16 or wider, within the bound.
A program may use at most 128 MiB of HBM per device.

v0:
```python
import jax
import jax.numpy as jnp
from jax import lax
from jax.sharding import PartitionSpec as P

KV_HEADS = 2
HEAD_DIM = 64


EPS = 1e-06


def side_by_side(arrays, axis, dim, along):
    widths = [a.shape[along] for a in arrays]
    both = jnp.concatenate(arrays, axis=along)
    filled = lax.all_gather(both, axis, axis=dim, tiled=True)
    return tuple(jnp.split(filled, [sum(widths[:k]) for k in range(1, len(widths))], axis=along))


def gathered_total(shard, axis):
    return lax.all_gather(shard, axis).astype(jnp.float32).sum(0)


def client_forward(tokens_in, gain_vec, query_w, keyval_w, output_w):
    x_float = tokens_in.astype(jnp.float32)
    inv_rms = lax.rsqrt(jnp.mean(x_float * x_float, axis=-1, keepdims=True) + EPS)
    normed = (x_float * inv_rms * gain_vec).astype(jnp.bfloat16)
    queries = jnp.dot(normed, query_w, preferred_element_type=jnp.float32).astype(jnp.bfloat16)
    key_vals = jnp.dot(normed, keyval_w, preferred_element_type=jnp.float32).astype(jnp.bfloat16)
    length = tokens_in.shape[0]
    half_cols = KV_HEADS * HEAD_DIM
    q_heads = queries.reshape(length, KV_HEADS, -1, HEAD_DIM)
    k_heads = key_vals[:, :half_cols].reshape(length, KV_HEADS, HEAD_DIM)
    v_heads = key_vals[:, half_cols:].reshape(length, KV_HEADS, HEAD_DIM)
    scores = jnp.einsum(
        "tgqd,sgd->gqts", q_heads, k_heads, preferred_element_type=jnp.float32
    ) * HEAD_DIM ** (-0.5)
    causal = jnp.arange(length)[:, None] >= jnp.arange(length)[None, :]
    scores = jnp.where(causal, scores, -1e30)
    highest = jnp.max(scores, axis=-1, keepdims=True)
    expo = jnp.exp(scores - highest)
    probs = (expo / jnp.sum(expo, axis=-1, keepdims=True)).astype(jnp.bfloat16)
    attended = jnp.einsum("gqts,sgd->tgqd", probs, v_heads, preferred_element_type=jnp.float32)
    attended = attended.astype(jnp.bfloat16).reshape(length, -1)
    mixed = jnp.dot(attended, output_w, preferred_element_type=jnp.float32)
    return (x_float + mixed).astype(jnp.bfloat16)


def norm_back(h_float, inv_rms, gain_vec, upstream):
    scaled = upstream * gain_vec
    return inv_rms * scaled - h_float * inv_rms**3 * jnp.mean(
        scaled * h_float, axis=-1, keepdims=True
    )


def on_device(
    client_input,
    client_gain,
    w_query,
    w_keyval,
    w_out,
    server_gain,
    w_gate,
    w_up,
    w_down,
    out_grad,
    valid,
):
    tokens_in = client_input[0, 0]
    gain_vec = client_gain[0]
    query_w = w_query[0]
    keyval_w = w_keyval[0]
    output_w = w_out[0]
    s_gain = server_gain[0]
    gate_w = w_gate[0]
    up_w = w_up[0]
    down_w = w_down[0]
    length = tokens_in.shape[0]
    width = tokens_in.shape[1]
    contract_last = (((1,), (1,)), ((), ()))
    contract_first = (((0,), (0,)), ((), ()))

    def client_part(query_in, keyval_in, output_in):
        return client_forward(tokens_in, gain_vec, query_in, keyval_in, output_in)

    own_cut, pull = jax.vjp(client_part, query_w, keyval_w, output_w)
    live = jnp.arange(length) < valid[0, 0]
    own_cot = jnp.where(live[:, None], out_grad[0, 0], jnp.zeros_like(out_grad[0, 0]))
    all_cut, all_cot = side_by_side((own_cut, own_cot), "mem", 0, 1)
    h_float = all_cut.astype(jnp.float32)
    inv_rms = lax.rsqrt(jnp.mean(h_float * h_float, axis=-1, keepdims=True) + EPS)
    normed = (h_float * inv_rms * s_gain).astype(jnp.bfloat16)
    gate_act = jnp.dot(normed, gate_w, preferred_element_type=jnp.float32)
    up_act = jnp.dot(normed, up_w, preferred_element_type=jnp.float32)
    sigma = jax.nn.sigmoid(gate_act)
    hidden = (gate_act * sigma * up_act).astype(jnp.bfloat16)
    served = lax.psum_scatter(
        jnp.dot(hidden, down_w, preferred_element_type=jnp.float32).astype(jnp.bfloat16),
        "mem",
        scatter_dimension=0,
        tiled=True,
    ).astype(jnp.float32)
    own_float = own_cut.astype(jnp.float32)
    server_out = (own_float + served).astype(jnp.bfloat16)
    d_hidden = lax.dot_general(all_cot, down_w, contract_last, preferred_element_type=jnp.float32)
    d_gate = (d_hidden * up_act * sigma * (1.0 + gate_act * (1.0 - sigma))).astype(jnp.bfloat16)
    d_up = (d_hidden * gate_act * sigma).astype(jnp.bfloat16)
    grad_down = lax.dot_general(
        hidden, all_cot, contract_first, preferred_element_type=jnp.float32
    ).astype(jnp.bfloat16)
    grad_gate = lax.dot_general(
        normed, d_gate, contract_first, preferred_element_type=jnp.float32
    ).astype(jnp.bfloat16)
    grad_up = lax.dot_general(
        normed, d_up, contract_first, preferred_element_type=jnp.float32
    ).astype(jnp.bfloat16)
    d_normed = lax.dot_general(d_gate, gate_w, contract_last, preferred_element_type=jnp.float32)
    d_normed = d_normed + lax.dot_general(
        d_up, up_w, contract_last, preferred_element_type=jnp.float32
    )
    pushed = norm_back(h_float, inv_rms, s_gain, d_normed)
    local_sum = jnp.sum(pushed.reshape(-1, length, width), axis=0) + own_cot.astype(jnp.float32)
    grad_total = gathered_total(local_sum.astype(jnp.bfloat16), "mem").astype(jnp.float32)
    cut_grad = (grad_total / lax.axis_size("mem")).astype(jnp.bfloat16)
    grad_q, grad_kv, grad_o = pull(cut_grad)
    summed = (
        lax.psum(grad_q.astype(jnp.float32).astype(jnp.bfloat16), "grp").astype(jnp.float32),
        lax.psum(grad_kv.astype(jnp.float32).astype(jnp.bfloat16), "grp").astype(jnp.float32),
        lax.psum(grad_o.astype(jnp.float32).astype(jnp.bfloat16), "grp").astype(jnp.float32),
    )
    groups = lax.axis_size("grp")
    grad_query = (summed[0] / groups).astype(jnp.bfloat16)
    grad_keyval = (summed[1] / groups).astype(jnp.bfloat16)
    grad_out = (summed[2] / groups).astype(jnp.bfloat16)
    return (
        server_out[None, None],
        grad_query[None],
        grad_keyval[None],
        grad_out[None],
        grad_gate[None],
        grad_up[None],
        grad_down[None],
    )


def solution(mesh):
    in_specs = (
        P("grp", "mem", None, None),
        P("mem", None),
        P("mem", None, None),
        P("mem", None, None),
        P("mem", None, None),
        P("grp", None),
        P("grp", None, "mem"),
        P("grp", None, "mem"),
        P("grp", "mem", None),
        P("grp", "mem", None, None),
        P("grp", "mem"),
    )
    out_specs = (
        P("grp", "mem", None, None),
        P("mem", None, None),
        P("mem", None, None),
        P("mem", None, None),
        P("grp", None, "mem"),
        P("grp", None, "mem"),
        P("grp", "mem", None),
    )
    return jax.shard_map(
        on_device, mesh=mesh, in_specs=in_specs, out_specs=out_specs, check_vma=False
    )
```

profile of v0, /device:TPU:1, one launch (start us, length us, event | category | flops | bytes accessed | tf_op | source)
XLA Modules:
  0.0 427.0 jit_solution(6634465796072064970)
XLA Ops:
  11.5 2.1 fusion.29
  17.4 77.5 %all-gather.3.cloned.1.call-done = bf16[2048,1792]{1,0:T(8,128)(2,1)} async-done(((bf16[128,1792]{1,0:T(8,128)(2,1)}), bf16[2048,1792]{1,0:T(8,128)(2,1)}) %all-gather.3.cloned.1.call-update) | async-done | bytes 7340048 | tf_op jit(solution)/shard_map/all_gather | solution.py:16
  95.0 2.8 fusion
  97.8 2.6 fusion.2
  105.3 3.5 multiply_convert_fusion.2
  108.8 2.3 fusion.59
  111.0 3.4 fusion.5
  114.5 3.8 fusion.4
  118.2 4.2 reduce_sum.95
  122.5 1.9 fusion.69
  124.6 5.6 %convolution_convert_fusion = bf16[2048,896]{1,0:T(8,128)(2,1)} fusion(bf16[2048,304]{0,1:T(8,128)(2,1)} %get-tuple-element.14, bf16[1,304,896]{2,1,0:T(8,128)(2,1)} %param.19), kind=kOutput, calls=%fused_computation.12 | convolution fusion | flops 1117519872 | bytes 5459968 | tf_op jit(solution)/shard_map/dot_general | solution.py:98
  131.0 50.8 %all-gather.5.cloned.1.call-done = bf16[16,128,896]{2,1,0:T(8,128)(2,1)} async-done(((bf16[1,128,896]{2,1,0:T(8,128)(2,1)}), bf16[16,128,896]{2,1,0:T(8,128)(2,1)}) %all-gather.5.cloned.1.call-update) | async-done | bytes 3670032 | tf_op jit(solution)/shard_map/all_gather | solution.py:21
  181.8 2.6 convert_reduce_fusion
  186.4 1.8 copy.37
  192.6 1.8 convolution_convert_fusion.2
  194.4 1.7 convolution_convert_fusion.1
  196.2 5.0 %fusion.22 = bf16[1,896,304]{1,2,0:T(8,128)(2,1)} fusion(bf16[2048,304]{0,1:T(8,128)(2,1)} %copy-done.11, bf16[2048,896]{1,0:T(8,128)(2,1)} %copy-done.4), kind=kOutput, calls=%fused_computation.43 | convolution fusion | flops 1115957248 | bytes 5459968 | tf_op jit(solution)/shard_map/dot_general | solution.py:114
  201.3 4.6 %fusion.21 = bf16[1,896,304]{1,2,0:T(8,128)(2,1)} fusion(bf16[2048,304]{0,1:T(8,128)(2,1)S(1)} %copy-done.6, bf16[2048,896]{1,0:T(8,128)(2,1)} %copy-done.4), kind=kOutput, calls=%fused_computation.42 | convolution fusion | flops 1115957248 | bytes 5459968 | tf_op jit(solution)/shard_map/dot_general | solution.py:111
  205.9 2.3 fusion.23
  208.2 60.4 %reduce-scatter.2.cloned.1.call-done = bf16[128,896]{1,0:T(8,128)(2,1)} async-done(((bf16[2048,896]{1,0:T(8,128)(2,1)}), bf16[128,896]{1,0:T(8,128)(2,1)}) %reduce-scatter.2.cloned.1.call-update) | async-done | bytes 229392 | tf_op jit(solution)/shard_map/reduce_scatter | solution.py:97
  268.6 1.7 fusion.72
  270.2 144.2 %all-reduce.5.cloned.1.call-done = (bf16[896,896]{1,0:T(8,128)(2,1)}, bf16[896,256]{1,0:T(8,128)(2,1)}, bf16[896,896]{1,0:T(8,128)(2,1)}) async-done(((bf16[896,896]{1,0:T(8,128)(2,1)}, bf16[896,256]{1,0:T(8,128)(2,1)}, bf16[896,896]{1,0:T(8,128)(2,1)}), (bf16[896,896]{1,0:T(8,128)(2,1)}, bf16[896,256]{1,0:T(8,128)(2,1)}, bf16[896,896]{1,0:T(8,128)(2,1)})) %all-reduce.5.cloned.1.call-update) | async-done | bytes 3670032 | tf_op jit(solution)/shard_map/psum | solution.py:127
  414.4 1.9 fusion.68
  416.3 4.2 fusion.10
  (98 shorter events, 19.3 us)
Async XLA Ops:
  7.2 8.0 %copy-start = (bf16[1,896,896]{2,1,0:T(8,128)(2,1)S(1)}, bf16[1,896,896]{2,1,0:T(8,128)(2,1)}, u32[]{:S(2)}) copy-start(bf16[1,896,896]{2,1,0:T(8,128)(2,1)} %param.15) | copy-start | bytes 4816900
  7.2 87.8 %all-gather.3.cloned.1.call-start = ((), (), s32[]{:S(2)}) async-start(), calls=%async_computation.1 | async-start | bytes 7798784 | tf_op jit(solution)/shard_map/all_gather | solution.py:16
  9.1 4.7 %copy-start.18 = (f32[128]{0:T(128)}, f32[128]{0:T(128)S(1)}, u32[]{:S(2)}) copy-start(f32[128]{0:T(128)S(1)} %add_rsqrt_fusion.1) | copy-start | bytes 1540
  9.8 4.0 copy-start.16
  14.8 2.6 copy-start.20
  17.2 164.6 %all-gather.5.cloned.1.call-start = ((), (), s32[]{:S(2)}) async-start(), calls=%async_computation.3 | async-start | bytes 3899392 | tf_op jit(solution)/shard_map/all_gather | solution.py:21
  97.8 2.6 copy-start.15
  100.5 1.9 copy-start.4
  100.5 1.9 copy-start.14
  100.5 3.7 slice-start
  102.4 2.9 slice-start.1
  102.4 2.9 copy-start.21
  108.7 2.3 copy-start.5
  108.7 2.3 copy-start.11
  124.4 144.2 %reduce-scatter.2.cloned.1.call-start = ((), (), s32[]{:S(2)}) async-start(), calls=%async_computation.2 | async-start | bytes 3899392 | tf_op jit(solution)/shard_map/reduce_scatter | solution.py:97
  130.3 284.1 %all-reduce.5.cloned.1.call-start = ((), (), s32[]{:S(2)}) async-start(), calls=%async_computation.4 | async-start | bytes 7340032 | tf_op jit(solution)/shard_map/psum | solution.py:127
  188.2 2.4 copy-start.10
  189.6 1.6 copy-start.17
  190.6 3.9 copy-start.3
  196.2 5.1 %copy-start.6 = (bf16[2048,304]{0,1:T(8,128)(2,1)S(1)}, bf16[2048,304]{0,1:T(8,128)(2,1)}, u32[]{:S(2)}) copy-start(bf16[2048,304]{0,1:T(8,128)(2,1)} %copy-done.5) | copy-start | bytes 3735556
  196.2 9.7 %slice-start.2 = ((s8[7340032]{0:T(1024)(128)(4,1)}), s8[4194304]{0:T(1024)(128)(4,1)S(1)}, s32[]{:S(2)}) async-start(s8[7340032]{0:T(1024)(128)(4,1)} %bitcast.184), calls=%async_computation.7 | async-start | bytes 8388608
  201.2 4.6 %slice-start.3 = ((s8[7340032]{0:T(1024)(128)(4,1)}), s8[3145728]{0:T(1024)(128)(4,1)S(1)}, s32[]{:S(2)}) async-start(s8[7340032]{0:T(1024)(128)(4,1)} %bitcast.184), calls=%async_computation.8 | async-start | bytes 6291456
  201.2 4.6 %copy-start.22 = (bf16[2048,304]{0,1:T(8,128)(2,1)S(1)}, bf16[2048,304]{0,1:T(8,128)(2,1)}, u32[]{:S(2)}) copy-start(bf16[2048,304]{0,1:T(8,128)(2,1)} %get-tuple-element.14) | copy-start | bytes 3735556
  205.9 62.7 %copy-start.8 = (bf16[128,896]{1,0:T(8,128)(2,1)S(1)}, bf16[128,896]{1,0:T(8,128)(2,1)}, u32[]{:S(2)}) copy-start(bf16[128,896]{1,0:T(8,128)(2,1)} %copy-done.7) | copy-start | bytes 688132
  (7 other events, 7.7 us)
Sparse Core Ops, SparseCore 0:
  17.3 77.6 all-gather.2
  124.5 57.2 all-gather.4
  186.1 82.3 reduce-scatter.1
  271.9 142.4 all-reduce.4
where the time goes:
time: 435 us; the launch traced here: 427 us
  waiting for transfers between devices  333 us (77%)
  matrix products  42.4 us (10%)
  other arithmetic  30.3 us (7%)
  between operations  15 us (3%)
  local copies, waits for them, and re-layouts  5.74 us (1%)
    psum x1, waiting for transfers between devices, on_device(): lax.psum(grad_q.astype(jnp.float32).astype(jnp.bfloat16), 'grp')  144 us
    all_gather x1, waiting for transfers between devices, side_by_side(): filled = lax.all_gather(both, axis, axis=dim, tiled=True)  77.5 us
    reduce_scatter x1, waiting for transfers between devices, on_device(): lax.psum_scatter(jnp.dot(hidden, down_w, preferred_element_type=jnp.float...  60.4 us
    all_gather x1, waiting for transfers between devices, gathered_total(): return lax.all_gather(shard, axis).astype(jnp.float32).sum(0)  50.8 us
  transfers between devices with their start and end apart: 4, of which 4 were waited for; matrix products, arithmetic and copies ran while one was open for 8% of the time, Pallas kernels for 0%

commit v1 on v0

v1 whole, which is shorter than its diff:
```python
import functools

import jax
import jax.numpy as jnp
from jax import lax
from jax.experimental import pallas as pl
from jax.experimental.pallas import tpu as pltpu
from jax.sharding import PartitionSpec as P

EPS = 1e-06
HEAD_DIM = 64
TOK = 128
D = 896
PAIRS = 7
BF = jnp.bfloat16
F32 = jnp.float32
MESH = pl.DeviceIdType.MESH
NN = (((1,), (0,)), ((), ()))
NT = (((1,), (1,)), ((), ()))
TN = (((0,), (0,)), ((), ()))
HALF = TOK // 2


def mm(a, b, dims=NN):
    return lax.dot_general(a, b, dims, preferred_element_type=F32)


def places():
    g, m = lax.axis_index("grp"), lax.axis_index("mem")
    l, z = g // 8, g % 8
    yh, x, c = m // 8, (m // 2) % 4, m % 2
    at = lambda y_, x_, c_: {"mem": y_ * 8 + x_ * 2 + c_}
    return dict(
        m=m,
        c=c,
        xp=at(yh, (x + 1) % 4, c),
        xm=at(yh, (x + 3) % 4, c),
        x2=at(yh, (x + 2) % 4, c),
        yp=at(1 - yh, x, c),
        yxp=at(1 - yh, (x + 1) % 4, c),
        yxm=at(1 - yh, (x + 3) % 4, c),
        yx2=at(1 - yh, (x + 2) % 4, c),
        co=at(yh, x, 1 - c),
        zp={"grp": l * 8 + (z + 1) % 8},
        zm={"grp": l * 8 + (z + 7) % 8},
        lp={"grp": (1 - l) * 8 + z},
    )


def remote(src, dst, send, recv, k, device):
    return pltpu.make_async_remote_copy(
        src_ref=src, dst_ref=dst, send_sem=send.at[k], recv_sem=recv.at[k], device_id=device, device_id_type=MESH
    )


def entry_barrier(devices):
    barrier = pltpu.get_barrier_semaphore()
    for device in devices:
        pl.semaphore_signal(barrier, inc=1, device_id=device, device_id_type=MESH)
    pl.semaphore_wait(barrier, len(devices))


def ring_slot(step, stream, way):
    return 2 + 4 * (step - 1) + 2 * stream + way if step < 4 else 14 + stream


def stacked_heads(both):
    wide = both.astype(F32)
    turned = pltpu.roll(wide, HEAD_DIM, 1)
    low = lax.broadcasted_iota(jnp.int32, wide.shape, 1) < HEAD_DIM
    zero = jnp.zeros_like(wide)
    first0, second0 = jnp.where(low, wide, zero), jnp.where(low, zero, turned)
    first1, second1 = jnp.where(low, turned, zero), jnp.where(low, zero, wide)
    pair = lambda a, b: jnp.concatenate([a, b], axis=0).astype(BF)
    return pair(first0, second0), pair(first0, second1), pair(first1, second1)


def of_pair(p, three):
    return three[0] if p < 3 else three[1] if p == 3 else three[2]


def client_forward(i, x, gain, wq_ref, wkv_ref, nt_ref, at_ref, q_ref, kv_ref, pt_ref, att_ref):
    xf = x.astype(F32)
    inv = lax.rsqrt(jnp.mean(xf * xf, axis=-1, keepdims=True) + EPS)
    normed_f = (xf * inv * gain).astype(BF)
    columns = pl.ds(pl.multiple_of(i * TOK, TOK), TOK)
    nt_ref[:, columns] = normed_f.T
    q_ref[i] = mm(normed_f, wq_ref[...]).astype(BF)
    kv = mm(normed_f, wkv_ref[...]).astype(BF)
    kv_ref[i] = kv
    keys, vals = stacked_heads(kv[:, :TOK]), stacked_heads(kv[:, TOK:])
    s_at = lax.broadcasted_iota(jnp.int32, (TOK, TOK), 0)
    t_at = lax.broadcasted_iota(jnp.int32, (TOK, TOK), 1)
    seen = s_at <= t_at
    for p in range(PAIRS):
        cols = slice(p * TOK, (p + 1) * TOK)
        scores = mm(of_pair(p, keys), q_ref[i, :, cols], NT) * HEAD_DIM ** (-0.5)
        halves = []
        for h in range(2):
            s = jnp.where(seen, scores[h * TOK : (h + 1) * TOK], -1e30)
            e = jnp.exp(s - jnp.max(s, axis=0, keepdims=True))
            halves.append((e / jnp.sum(e, axis=0, keepdims=True)).astype(BF))
        pt = jnp.concatenate(halves, axis=0)
        pt_ref[i, p] = pt
        att_ref[:, cols] = mm(pt, of_pair(p, vals), TN).astype(BF)
    at_ref[:, columns] = att_ref[...].T
    return xf


def gather_kernel(
    x_ref, cot_ref, gain_ref, wq_ref, wkv_ref, wo_ref, wg_ref, wu_ref, wd_ref,
    cut_ref, allcot_ref, nt_ref, at_ref, q_ref, kv_ref, pt_ref, pg_ref, pu_ref, pd_ref,
    xs_ref, att_ref, send_m, recv_m, send_z, recv_z, send_w, recv_w,
):
    pos = places()
    entry_barrier([pos[k] for k in ("xp", "xm", "yp", "co", "zp", "zm", "lp")])
    lo, hi = pl.ds(0, HALF), pl.ds(HALF, HALF)

    def mem_copies(base, all_ref, own):
        plan = [
            (own, all_ref.at[1], "xp"),
            (own, all_ref.at[2], "xm"),
            (own, all_ref.at[4], "yp"),
            (all_ref.at[1, lo], all_ref.at[3, lo], "xp"),
            (all_ref.at[2, hi], all_ref.at[3, hi], "xm"),
            (all_ref.at[4], all_ref.at[5], "xp"),
            (all_ref.at[4], all_ref.at[6], "xm"),
            (all_ref.at[5, lo], all_ref.at[7, lo], "xp"),
            (all_ref.at[6, hi], all_ref.at[7, hi], "xm"),
        ]
        return [remote(s, d, send_m, recv_m, base + k, pos[n]) for k, (s, d, n) in enumerate(plan)]

    cot = mem_copies(0, allcot_ref, cot_ref)
    cut = mem_copies(9, cut_ref, cut_ref.at[0])

    ring = {}
    for stream in range(2):
        for way, name in ((0, "zp"), (1, "zm")):
            for step in range(1, 5):
                src = x_ref if stream == 0 else xs_ref.at[1]
                if step > 1:
                    src = xs_ref.at[ring_slot(step - 1, stream, way)]
                dst = xs_ref.at[ring_slot(step, stream, way)]
                if step == 4:
                    part = (lo, hi)[way]
                    src, dst = src.at[part], dst.at[part]
                k = 1 + (step - 1) * 4 + stream * 2 + way
                ring[step, stream, way] = remote(src, dst, send_z, recv_z, k, pos[name])
    across = remote(x_ref, xs_ref.at[1], send_z, recv_z, 0, pos["lp"])
    swap = [
        remote(s, d, send_w, recv_w, k, pos["co"])
        for k, (s, d) in enumerate(((wg_ref, pg_ref), (wu_ref, pu_ref), (wd_ref, pd_ref)))
    ]

    across.start()
    for copy in cot[:3] + [ring[1, 0, 0], ring[1, 0, 1]] + swap:
        copy.start()
    allcot_ref[0] = cot_ref[...]
    gain = gain_ref[...]
    saved = (nt_ref, at_ref, q_ref, kv_ref, pt_ref, att_ref)
    xf = client_forward(0, x_ref[...], gain, wq_ref, wkv_ref, *saved)
    cut_ref[0] = (xf + mm(att_ref[...], wo_ref[...])).astype(BF)
    for copy in cut[:3]:
        copy.start()

    def from_neighbours(copies):
        copies[0].wait_recv()
        copies[3].start()
        copies[1].wait_recv()
        copies[4].start()

    def from_across(copies):
        copies[2].wait_recv()
        copies[5].start()
        copies[6].start()

    def from_far(copies):
        copies[5].wait_recv()
        copies[7].start()
        copies[6].wait_recv()
        copies[8].start()

    def on_ring(step, stream):
        for way in range(2):
            ring[step, stream, way].wait_recv()
            if step < 4:
                ring[step + 1, stream, way].start()

    def first():
        across.wait_recv()
        ring[1, 1, 0].start()
        ring[1, 1, 1].start()
        from_neighbours(cot)
        from_across(cot)

    events = {
        1: [first],
        2: [lambda: on_ring(1, 0)],
        3: [lambda: from_neighbours(cut), lambda: from_across(cut)],
        4: [lambda: on_ring(1, 1)],
        5: [lambda: from_far(cot)],
        6: [lambda: on_ring(2, 0)],
        7: [lambda: from_far(cut)],
        8: [lambda: on_ring(2, 1)],
        10: [lambda: on_ring(3, 0)],
        12: [lambda: on_ring(3, 1)],
        14: [lambda: on_ring(4, 0)],
        15: [lambda: on_ring(4, 1)],
    }

    @pl.loop(1, 16)
    def _(i):
        for at, todo in events.items():
            @pl.when(i == at)
            def _():
                for act in todo:
                    act()

        client_forward(i, xs_ref[i], gain, wq_ref, wkv_ref, *saved)

    for copies in (cot, cut):
        for k in (3, 4, 7, 8):
            copies[k].wait_recv()
    for copy in swap:
        copy.wait_recv()
    for copy in cot + cut + list(ring.values()) + [across] + swap:
        copy.wait_send()


def gather_call(x, cot, gain, wq, wkv, wo, wg, wu, wd):
    vmem, anyspace = pl.BlockSpec(memory_space=pltpu.VMEM), pl.BlockSpec(memory_space=pl.ANY)
    sds = jax.ShapeDtypeStruct
    return pl.pallas_call(
        gather_kernel,
        out_shape=(
            sds((8, TOK, D), BF), sds((8, TOK, D), BF), sds((D, 16 * TOK), BF), sds((D, 16 * TOK), BF),
            sds((16, TOK, D), BF), sds((16, TOK, 2 * TOK), BF), sds((16, PAIRS, 2 * TOK, TOK), BF),
            sds(wg.shape, BF), sds(wu.shape, BF), sds(wd.shape, BF),
        ),
        in_specs=[vmem] * 6 + [anyspace] * 3,
        out_specs=[vmem] * 7 + [anyspace] * 3,
        scratch_shapes=[
            pltpu.VMEM((16, TOK, D), BF), pltpu.VMEM((TOK, D), BF),
            pltpu.SemaphoreType.DMA((18,)), pltpu.SemaphoreType.DMA((18,)),
            pltpu.SemaphoreType.DMA((17,)), pltpu.SemaphoreType.DMA((17,)),
            pltpu.SemaphoreType.DMA((3,)), pltpu.SemaphoreType.DMA((3,)),
        ],
        compiler_params=pltpu.CompilerParams(collective_id=0, has_side_effects=True, vmem_limit_bytes=56 * 2**20),
        name="gather_forward",
    )(x, cot, gain, wq, wkv, wo, wg, wu, wd)


def client_backward(i, cg, wo_ref, q_ref, kv_ref, pt_ref, dq_ref, dkv_ref, datt_ref):
    datt_ref[...] = mm(cg, wo_ref[...], NT).astype(BF)
    kv = kv_ref[i]
    keys, vals = stacked_heads(kv[:, :TOK]), stacked_heads(kv[:, TOK:])
    rows = pl.ds(pl.multiple_of(i * TOK, TOK), TOK)
    sums = {}

    def add(key, value):
        sums[key] = value if key not in sums else sums[key] + value

    for p in range(PAIRS):
        cols = slice(p * TOK, (p + 1) * TOK)
        d_out = datt_ref[:, cols]
        pt = pt_ref[i, p]
        d_probs = mm(of_pair(p, vals), d_out, NT)
        wide = pt.astype(F32)
        halves = []
        for h in range(2):
            half = slice(h * TOK, (h + 1) * TOK)
            both = d_probs[half] * wide[half]
            halves.append((both - wide[half] * jnp.sum(both, axis=0, keepdims=True)) * HEAD_DIM ** (-0.5))
        ds = jnp.concatenate(halves, axis=0).astype(BF)
        dq_ref[rows, cols] = mm(ds, of_pair(p, keys), TN).astype(BF)
        dk, dv = mm(ds, q_ref[i, :, cols]), mm(pt, d_out)
        for h in range(2):
            kv_head = (2 * p + h) // PAIRS
            half = slice(h * TOK, (h + 1) * TOK)
            add(("k", kv_head, h), dk[half])
            add(("v", kv_head, h), dv[half])
    low = lax.broadcasted_iota(jnp.int32, (TOK, TOK), 1) < HEAD_DIM
    for at, name in enumerate(("k", "v")):
        first = sums[name, 0, 0] + pltpu.roll(sums[name, 0, 1], HEAD_DIM, 1)
        second = sums[name, 1, 1] + pltpu.roll(sums[name, 1, 0], HEAD_DIM, 1)
        dkv_ref[rows, at * TOK : (at + 1) * TOK] = jnp.where(low, first, second).astype(BF)


def back_kernel(
    ls_ref, served_ref, cut_ref, og_ref, ou_ref, od_ref, nt_ref, at_ref, q_ref, kv_ref, pt_ref, wo_ref,
    out_ref, gq_ref, gkv_ref, go_ref, pg_ref, pu_ref, pd_ref,
    part_ref, mine_ref, slices_ref, cg_ref, got_ref, dq_ref, dkv_ref, datt_ref,
    send_r, recv_r, send_a, recv_a, send_z, recv_z, send_c, recv_c, send_s, recv_s, send_w, recv_w,
):
    pos = places()
    m, c = pos["m"], pos["c"]
    peers = [{"mem": (m + d) % 16} for d in range(1, 16)]
    entry_barrier(peers + [pos[k] for k in ("zp", "zm", "lp")])

    shares = [
        remote(ls_ref.at[(m + d) % 16], part_ref.at[d - 1], send_r, recv_r, d - 1, peers[d - 1]) for d in range(1, 16)
    ]
    for copy in shares:
        copy.start()
    total = ls_ref[m].astype(F32)
    for d in range(15):
        shares[d].wait_recv()
        total = total + part_ref[d].astype(F32)
    mine_ref[...] = (total * (1.0 / 16)).astype(BF)
    spread = [remote(mine_ref, slices_ref.at[m], send_a, recv_a, d, peers[d]) for d in range(15)]
    for copy in spread:
        copy.start()
    slices_ref[m] = mine_ref[...]
    for d in range(15):
        spread[d].wait_recv()
    cg_ref[0] = slices_ref[...].astype(F32).reshape(TOK, D).astype(BF)

    def part(slot, start, size):
        return cg_ref.at[slot, pl.ds(pl.multiple_of(c * HALF + start, 32), size)]

    ring, over = {}, {}
    for stream in range(2):
        for way, name in ((0, "zp"), (1, "zm")):
            for step in range(1, 5):
                before = stream if step == 1 else ring_slot(step - 1, stream, way)
                after = ring_slot(step, stream, way)
                span = (0, HALF) if step < 4 else (way * 32, 32)
                k = 1 + (step - 1) * 4 + stream * 2 + way
                ring[step, stream, way] = remote(part(before, *span), part(after, *span), send_z, recv_z, k, pos[name])
    across = remote(part(0, 0, HALF), part(1, 0, HALF), send_z, recv_z, 0, pos["lp"])
    for slot in range(1, 16):
        over[slot] = remote(part(slot, 0, HALF), part(slot, 0, HALF), send_c, recv_c, slot - 1, pos["co"])
    across.start()
    ring[1, 0, 0].start()
    ring[1, 0, 1].start()
    names = ("xm", "xp", "x2", "yp", "yxm", "yxp", "yx2")
    serve = [remote(served_ref.at[k + 1], got_ref.at[k], send_s, recv_s, k, pos[n]) for k, n in enumerate(names)]
    swap = [
        remote(s, d, send_w, recv_w, k, pos["co"])
        for k, (s, d) in enumerate(((og_ref, pg_ref), (ou_ref, pu_ref), (od_ref, pd_ref)))
    ]
    for copy in serve + swap:
        copy.start()

    def on_ring(step, stream):
        for way in range(2):
            ring[step, stream, way].wait_recv()
            if step < 4:
                ring[step + 1, stream, way].start()
                over[ring_slot(step, stream, way)].start()
        if step == 4:
            over[14 + stream].start()

    def first():
        across.wait_recv()
        ring[1, 1, 0].start()
        ring[1, 1, 1].start()
        over[1].start()
        on_ring(1, 0)
        over[1].wait_recv()

    def handed(*slots):
        for slot in slots:
            over[slot].wait_recv()

    events = {
        1: [first],
        2: [lambda: on_ring(1, 1), lambda: handed(2, 3)],
        4: [lambda: on_ring(2, 0), lambda: handed(4, 5)],
        6: [lambda: on_ring(2, 1), lambda: handed(6, 7)],
        8: [lambda: on_ring(3, 0), lambda: handed(8, 9)],
        10: [lambda: on_ring(3, 1), lambda: handed(10, 11)],
        12: [lambda: on_ring(4, 0), lambda: on_ring(4, 1), lambda: handed(12, 13)],
        14: [lambda: handed(14, 15)],
    }

    @pl.loop(0, 16)
    def _(i):
        for at, todo in events.items():
            @pl.when(i == at)
            def _():
                for act in todo:
                    act()

        client_backward(i, cg_ref[i], wo_ref, q_ref, kv_ref, pt_ref, dq_ref, dkv_ref, datt_ref)

    @pl.loop(0, 7)
    def _(t):
        rows = pl.ds(pl.multiple_of(t * TOK, TOK), TOK)
        gq_ref[rows, :] = (mm(nt_ref[rows, :], dq_ref[...]) * (1.0 / 16)).astype(BF)
        gkv_ref[rows, :] = (mm(nt_ref[rows, :], dkv_ref[...]) * (1.0 / 16)).astype(BF)
        go_ref[rows, :] = (mm(at_ref[rows, :], cg_ref[...].reshape(16 * TOK, D)) * (1.0 / 16)).astype(BF)

    for copy in serve:
        copy.wait_recv()
    out = cut_ref[...].astype(F32) + served_ref[0].astype(F32)
    for k in range(7):
        out = out + got_ref[k].astype(F32)
    out_ref[...] = out.astype(BF)
    for copy in swap:
        copy.wait_recv()
    for copy in shares + spread + list(ring.values()) + [across] + list(over.values()) + serve + swap:
        copy.wait_send()


def back_call(ls, served, cut, og, ou, od, nt, at, q, kv, pt, wo):
    vmem, anyspace = pl.BlockSpec(memory_space=pltpu.VMEM), pl.BlockSpec(memory_space=pl.ANY)
    sds = jax.ShapeDtypeStruct
    sem = pltpu.SemaphoreType.DMA
    return pl.pallas_call(
        back_kernel,
        out_shape=(
            sds((TOK, D), BF), sds((D, D), BF), sds((D, 2 * TOK), BF), sds((D, D), BF),
            sds(og.shape, BF), sds(ou.shape, BF), sds(od.shape, BF),
        ),
        in_specs=[vmem] * 3 + [anyspace] * 3 + [vmem] * 6,
        out_specs=[vmem] * 4 + [anyspace] * 3,
        scratch_shapes=[
            pltpu.VMEM((15, 8, D), BF), pltpu.VMEM((8, D), BF), pltpu.VMEM((16, 8, D), BF),
            pltpu.VMEM((16, TOK, D), BF), pltpu.VMEM((7, TOK, D), BF),
            pltpu.VMEM((16 * TOK, D), BF), pltpu.VMEM((16 * TOK, 2 * TOK), BF), pltpu.VMEM((TOK, D), BF),
            sem((15,)), sem((15,)), sem((15,)), sem((15,)), sem((17,)), sem((17,)), sem((15,)), sem((15,)),
            sem((7,)), sem((7,)), sem((3,)), sem((3,)),
        ],
        compiler_params=pltpu.CompilerParams(collective_id=1, has_side_effects=True, vmem_limit_bytes=56 * 2**20),
        name="cut_grad_backward",
    )(ls, served, cut, og, ou, od, nt, at, q, kv, pt, wo)


def server(cuts, cots, s_gain, gate_w, up_w, down_w):
    rows = cuts.reshape(-1, D)
    cot = cots.reshape(-1, D)
    h_float = rows.astype(F32)
    inv_rms = lax.rsqrt(jnp.mean(h_float * h_float, axis=-1, keepdims=True) + EPS)
    normed = (h_float * inv_rms * s_gain).astype(BF)
    gate_act, up_act = mm(normed, gate_w), mm(normed, up_w)
    sigma = jax.nn.sigmoid(gate_act)
    hidden = (gate_act * sigma * up_act).astype(BF)
    served = mm(hidden, down_w).astype(BF).reshape(cuts.shape)
    d_hidden = mm(cot, down_w, NT)
    d_gate = (d_hidden * up_act * sigma * (1.0 + gate_act * (1.0 - sigma))).astype(BF)
    d_up = (d_hidden * gate_act * sigma).astype(BF)
    d_normed = mm(d_gate, gate_w, NT) + mm(d_up, up_w, NT)
    scaled = d_normed * s_gain
    pushed = inv_rms * scaled - h_float * inv_rms**3 * jnp.mean(scaled * h_float, axis=-1, keepdims=True)
    local_sum = jnp.sum(pushed.reshape(cuts.shape), axis=0) + cots[0].astype(F32)
    return served, local_sum.astype(BF), mm(normed, d_gate, TN), mm(normed, d_up, TN), mm(hidden, cot, TN)


def on_device(
    client_input, client_gain, w_query, w_keyval, w_out, server_gain, w_gate, w_up, w_down, out_grad, valid
):
    live = jnp.arange(TOK) < valid[0, 0]
    cot = jnp.where(live[:, None], out_grad[0, 0], jnp.zeros_like(out_grad[0, 0]))
    gate_w, up_w, down_w = w_gate[0], w_up[0], w_down[0]
    width = gate_w.shape[1]
    cuts, cots, nt, at, q, kv, pt, far_gate, far_up, far_down = gather_call(
        client_input[0, 0], cot, client_gain, w_query[0], w_keyval[0], w_out[0], gate_w, up_w, down_w
    )
    served, local_sum, gg, gu, gd = server(
        cuts,
        cots,
        server_gain[0],
        jnp.concatenate([gate_w, far_gate], axis=1),
        jnp.concatenate([up_w, far_up], axis=1),
        jnp.concatenate([down_w, far_down], axis=0),
    )
    server_out, grad_q, grad_kv, grad_o, rg, ru, rd = back_call(
        local_sum.reshape(16, 8, D),
        served,
        cuts[0],
        gg[:, width:].astype(BF),
        gu[:, width:].astype(BF),
        gd[width:].astype(BF),
        nt, at, q, kv, pt, w_out[0],
    )
    join = lambda own, got: (own + got.astype(F32)).astype(BF)[None]
    return (
        server_out[None, None],
        grad_q[None],
        grad_kv[None],
        grad_o[None],
        join(gg[:, :width], rg),
        join(gu[:, :width], ru),
        join(gd[:width], rd),
    )


def solution(mesh):
    in_specs = (
        P("grp", "mem", None, None),
        P("mem", None),
        P("mem", None, None),
        P("mem", None, None),
        P("mem", None, None),
        P("grp", None),
        P("grp", None, "mem"),
        P("grp", None, "mem"),
        P("grp", "mem", None),
        P("grp", "mem", None, None),
        P("grp", "mem"),
    )
    out_specs = (
        P("grp", "mem", None, None),
        P("mem", None, None),
        P("mem", None, None),
        P("mem", None, None),
        P("grp", None, "mem"),
        P("grp", None, "mem"),
        P("grp", "mem", None),
    )
    return jax.shard_map(
        on_device, mesh=mesh, in_specs=in_specs, out_specs=out_specs, check_vma=False
    )
```

time: 435 us -> 205 us (0.47); the launches traced: 427 us -> 205 us
  waiting for transfers between devices: 333 us -> 0 us
  Pallas kernels: 0 us -> 144 us
  matrix products: 42.4 us -> 23.4 us
  other arithmetic: 30.3 us -> 14.5 us
  local copies, waits for them, and re-layouts: 5.74 us -> 21.1 us
  between operations: 15 us -> 1.62 us
    psum x1 -> x0, waiting for transfers between devices: 144 us -> none  [on_device(): lax.psum(grad_q.astype(jnp.float32).astype(jnp.bfloat16), 'grp')]
    pallas_call x0 -> x2, Pallas kernels: none -> 144 us  [the longest x1 82 us: back_call(): pl.pallas_call(back_kernel, out_shape=(sds((TOK, D), BF), sds((D, D), BF)...]
    all_gather x2 -> x0, waiting for transfers between devices: 128 us -> none  [the longest x1 77.5 us: side_by_side(): filled = lax.all_gather(both, axis, axis=dim, tiled=True)]
    reduce_scatter x1 -> x0, waiting for transfers between devices: 60.4 us -> none  [on_device(): lax.psum_scatter(jnp.dot(hidden, down_w, preferred_element_type=jnp.float...]
    dot_general x22 -> x9, matrix products: 42.4 us -> 23.4 us  [mm(): return lax.dot_general(a, b, dims, preferred_element_type=F32)]
    unnamed x54 -> x64, local copies, waits for them, and re-layouts: 3.57 us -> 19.2 us
    reduce_sum x6 -> x2, other arithmetic: 11.3 us -> 4.32 us  [the longest x1 2.26 us: server(): jnp.sum(pushed.reshape(cuts.shape), axis=0) + cots[0].astype(F32)]
  transfers between devices with their start and end apart: 4 -> 0, of which waited for: 4 -> 0; matrix products, arithmetic and copies ran while one was open for 8% -> 0% of each run, Pallas kernels for 0% -> 0%
where the time goes in v1:
time: 205 us
  Pallas kernels  144 us (70%)
  matrix products  23.4 us (11%)
  local copies, waits for them, and re-layouts  21.1 us (10%)
  other arithmetic  14.5 us (7%)
    pallas_call x1, Pallas kernels, back_call(): pl.pallas_call(back_kernel, out_shape=(sds((TOK, D), BF), sds((D, D), BF)...  82 us
    pallas_call x1, Pallas kernels, gather_call(): pl.pallas_call(gather_kernel, out_shape=(sds((8, TOK, D), BF), sds((8, TO...  62 us
    dot_general x9, matrix products, mm(): return lax.dot_general(a, b, dims, preferred_element_type=F32)  23.4 us
    unnamed x64, local copies, waits for them, and re-layouts  19.2 us

profile of v1, /device:TPU:1, one launch (start us, length us, event | category | flops | bytes accessed | tf_op | source)
XLA Modules:
  0.0 204.7 jit_solution(10837038715715977640)
XLA Ops:
  1.4 1.7 bitcast_select_fusion.cot_ref
  3.1 2.2 %copy.26 = bf16[1,896,304]{2,1,0:T(8,128)(2,1)} copy(bf16[1,896,304]{1,2,0:T(8,128)(2,1)} %param.17) | data formatting | bytes 1089536 | tf_op args[6]
  6.4 62.0 %gather_forward.1 = (bf16[8,128,896]{2,1,0:T(8,128)(2,1)}, bf16[8,128,896]{2,1,0:T(8,128)(2,1)}, bf16[896,2048]{1,0:T(8,128)(2,1)}, bf16[896,2048]{1,0:T(8,128)(...) custom-call(bf16[128,896]{1,0:T(8,128)(2,1)} %bitcast.80, ...), custom_call_target="tpu_custom_call" | custom-call | tf_op jit(solution)/shard_map/gather_forward/pallas_call | solution.py:233
  68.5 2.1 %fusion = f32[8,128]{1,0:T(8,128)S(1)} fusion(bf16[8,128,896]{2,1,0:T(8,128)(2,1)} %get-tuple-element.24), kind=kLoop, calls=%fused_computation.4 | loop fusion | flops 2751488 | bytes 1839104 | tf_op jit(solution)/shard_map/reduce_sum | solution.py:434
  71.9 1.5 fusion.11
  73.6 1.5 fusion.7
  75.1 4.5 %multiply_convert_fusion = (bf16[1024,608]{0,1:T(8,128)(2,1)}, bf16[1024,608]{0,1:T(8,128)(2,1)S(1)}, bf16[1024,608]{0,1:T(8,128)(2,1)S(1)}) fusion(f32[1024,608]{0,1:T(8,128)S(1)} %fusion.11, f32[1024,608]{0,1:T(8,128)S(1)} %fusion.7, bf16[1024,896]{1,0:T(8,128)(2,1)S(1)} %fusion.2, bf16[896,304]{1,0:T(8,128)(2,1)S(1)} %copy-done.14, ...), kind=kOutput, calls=%fused_computation.11 | convolution fusion | flops 1127825408 | bytes 11640832 | tf_op jit(solution)/shard_map/dot_general | solution.py:25
  79.6 1.9 fusion.10
  81.6 2.5 %fusion.5 = (f32[1024]{0:T(1024)S(1)}, f32[1024,896]{1,0:T(8,128)S(1)}) fusion(bf16[8,128,896]{2,1,0:T(8,128)(2,1)S(1)} %copy-done, f32[896]{0:T(1024)S(1)} %reduce.1, f32[1024,896]{1,0:T(8,128)S(1)} %fusion.10, bf16[1024,608]{0,1:T(8,128)(2,1)S(1)} %get-tuple-element.57, bf16[896,304]{1,0:T(8,128)(2,1)S(1)} %copy-done.14, bf16[896,304]{1,0:T(8,128)(2,1)S(1)} %bitcast.66), kind=kOutput, calls=%fused_computation.9 | convolution fusion | flops 1122450432 | bytes 11517440 | tf_op jit(solution)/shard_map/dot_general | solution.py:25
  84.1 2.4 %fusion.4 = f32[1024,896]{1,0:T(8,128)} fusion(bf16[8,128,896]{2,1,0:T(8,128)(2,1)S(1)} %copy-done, f32[1024,896]{1,0:T(8,128)S(1)} %get-tuple-element.59, f32[1024]{0:T(1024)S(1)} %get-tuple-element.61, f32[1024]{0:T(1024)S(1)} %get-tuple-element.60, f32[1024]{0:T(1024)S(1)} %rsqrt_bitcast_fusion), kind=kLoop, calls=%fused_computation.8 | loop fusion | flops 4587520 | bytes 9187328 | tf_op jit(solution)/shard_map/sub | solution.py:445
  86.5 2.3 %reduce_sum.31 = f32[128,896]{1,0:T(8,128)S(1)} reduce(f32[8,128,896]{2,1,0:T(8,128)} %bitcast.61, f32[]{:T(128)} %constant.3.clone.1), dimensions={0}, to_apply=%region_2.3 | reduce | flops 802816 | bytes 4128772 | tf_op jit(solution)/shard_map/reduce_sum | solution.py:446
  88.8 1.7 fusion.14.ls_ref
  90.4 4.5 %convolution_convert_fusion = bf16[1024,896]{1,0:T(8,128)(2,1)} fusion(bf16[1024,608]{0,1:T(8,128)(2,1)} %get-tuple-element.55, bf16[304,896]{1,0:T(8,128)(2,1)S(1)} %copy-done.23, bf16[304,896]{1,0:T(8,128)(2,1)S(1)} %bitcast.76), kind=kOutput, calls=%fused_computation.15 | convolution fusion | flops 1118781440 | bytes 4169728 | tf_op jit(solution)/shard_map/dot_general | solution.py:25
  95.7 1.5 fusion.22
  97.1 1.3 copy-done.11
  100.2 2.8 %fusion.23 = f32[896,608]{0,1:T(8,128)S(1)} fusion(bf16[1024,608]{0,1:T(8,128)(2,1)} %copy-done.9, bf16[1024,896]{1,0:T(8,128)(2,1)S(1)} %copy-done.6), kind=kOutput, calls=%fused_computation.49 | convolution fusion | flops 1115684864 | bytes 5259264 | tf_op jit(solution)/shard_map/dot_general | solution.py:25
  103.0 1.3 copy-done.2
  106.1 2.8 %fusion.21 = f32[608,896]{1,0:T(8,128)S(1)} fusion(bf16[1024,608]{0,1:T(8,128)(2,1)} %get-tuple-element.55, bf16[1024,896]{1,0:T(8,128)(2,1)S(1)} %bitcast.82), kind=kOutput, calls=%fused_computation.47 | convolution fusion | flops 1115684864 | bytes 5259264 | tf_op jit(solution)/shard_map/dot_general | solution.py:25
  108.8 1.4 copy-done.10
  111.0 82.0 %cut_grad_backward.1 = (bf16[128,896]{1,0:T(8,128)(2,1)}, bf16[896,896]{1,0:T(8,128)(2,1)}, bf16[896,256]{1,0:T(8,128)(2,1)}, bf16[896,896]{1,0:T(8,128)(2,1)}, ...) custom-call(bf16[16,8,896]{2,1,0:T(8,128)(2,1)} %fusion.14.ls_ref, ...), custom_call_target="tpu_custom_call" | custom-call | tf_op jit(solution)/shard_map/cut_grad_backward/pallas_call | solution.py:410
  193.6 1.2 fusion.8
  198.4 2.4 %fusion.13 = bf16[1,304,896]{2,1,0:T(8,128)(2,1)} fusion(bf16[304,896]{1,0:T(8,128)(2,1)} %get-tuple-element.40, f32[608,896]{1,0:T(8,128)} %copy-done.10), kind=kLoop, calls=%fused_computation.32 | loop fusion | flops 817152 | bytes 2179072 | tf_op jit(solution)/shard_map/broadcast_in_dim | solution.py:477
  201.5 1.2 copy.44
  203.5 1.2 copy.46
  (71 shorter events, 13.3 us)
Async XLA Ops:
  0.6 4.6 %copy-start.15 = (bf16[1,896,304]{1,2,0:T(8,128)(2,1)S(1)}, bf16[1,896,304]{1,2,0:T(8,128)(2,1)}, u32[]{:S(2)}) copy-start(bf16[1,896,304]{1,2,0:T(8,128)(2,1)} %param.18) | copy-start | bytes 1634308
  6.4 62.0 %copy-start.21 = (f32[1,896]{1,0:T(1,128)S(1)}, f32[1,896]{1,0:T(1,128)}, u32[]{:S(2)}) copy-start(f32[1,896]{1,0:T(1,128)} %param.16) | copy-start | bytes 10756
  68.4 2.1 %copy-start = (bf16[8,128,896]{2,1,0:T(8,128)(2,1)S(1)}, bf16[8,128,896]{2,1,0:T(8,128)(2,1)}, u32[]{:S(2)}) copy-start(bf16[8,128,896]{2,1,0:T(8,128)(2,1)} %get-tuple-element.24) | copy-start | bytes 5505028
  70.5 1.3 copy-start.22
  71.1 4.1 %copy-start.4 = (bf16[1024,896]{1,0:T(8,128)(2,1)}, bf16[1024,896]{1,0:T(8,128)(2,1)S(1)}, u32[]{:S(2)}) copy-start(bf16[1024,896]{1,0:T(8,128)(2,1)S(1)} %fusion.2) | copy-start | bytes 5505028
  71.8 1.5 copy-start.16
  71.8 1.7 copy-start.19
  71.8 1.8 copy-start.23
  73.6 1.5 copy-start.1
  73.6 1.5 copy-start.14
  79.6 2.0 copy-start.24
  79.6 2.0 copy-start.9
  90.4 5.2 %copy-start.5 = (bf16[1024,896]{1,0:T(8,128)(2,1)S(1)}, bf16[1024,896]{1,0:T(8,128)(2,1)}, u32[]{:S(2)}) copy-start(bf16[1024,896]{1,0:T(8,128)(2,1)} %copy-done.4) | copy-start | bytes 5505028
  90.4 5.2 %copy-start.25 = (bf16[1024,608]{0,1:T(8,128)(2,1)S(1)}, bf16[1024,608]{0,1:T(8,128)(2,1)}, u32[]{:S(2)}) copy-start(bf16[1024,608]{0,1:T(8,128)(2,1)} %copy-done.24) | copy-start | bytes 3735556
  97.1 1.3 copy-start.11
  98.4 1.7 copy-start.6
  103.0 1.4 copy-start.2
  104.3 1.7 copy-start.20
  108.8 1.4 copy-start.10
  111.0 82.1 %copy-start.12 = (f32[896,608]{0,1:T(8,128)S(1)}, f32[896,608]{0,1:T(8,128)}, u32[]{:S(2)}) copy-start(f32[896,608]{0,1:T(8,128)} %copy-done.11) | copy-start | bytes 6537220
  197.3 3.5 %copy-start.18 = (bf16[128,896]{1,0:T(8,128)(2,1)S(1)}, bf16[128,896]{1,0:T(8,128)(2,1)}, u32[]{:S(2)}) copy-start(bf16[128,896]{1,0:T(8,128)(2,1)} %get-tuple-element.34) | copy-start | bytes 688132
  198.4 3.1 %copy-start.8 = (bf16[896,896]{1,0:T(8,128)(2,1)S(1)}, bf16[896,896]{1,0:T(8,128)(2,1)}, u32[]{:S(2)}) copy-start(bf16[896,896]{1,0:T(8,128)(2,1)} %get-tuple-element.35) | copy-start | bytes 4816900
  200.8 1.9 copy-start.17
  201.5 2.0 copy-start.7
  (3 other events, 3.5 us)

commit v2 on v0

v2 whole, which is shorter than its diff:
```python
import functools

import jax
import jax.numpy as jnp
from jax import lax
from jax.experimental import pallas as pl
from jax.experimental.pallas import tpu as pltpu
from jax.sharding import PartitionSpec as P

EPS = 1e-06
HEAD_DIM = 64
TOK = 128
D = 896
PAIRS = 7
BF = jnp.bfloat16
F32 = jnp.float32
MESH = pl.DeviceIdType.MESH
NN = (((1,), (0,)), ((), ()))
NT = (((1,), (1,)), ((), ()))
TN = (((0,), (0,)), ((), ()))
HALF = TOK // 2
SCALE = HEAD_DIM ** (-0.5)


def mm(a, b, dims=NN):
    return lax.dot_general(a, b, dims, preferred_element_type=F32)


def places():
    g, m = lax.axis_index("grp"), lax.axis_index("mem")
    l, z = g // 8, g % 8
    yh, x, c = m // 8, (m // 2) % 4, m % 2
    at = lambda y_, x_, c_: {"mem": y_ * 8 + x_ * 2 + c_}
    return dict(
        m=m,
        c=c,
        xp=at(yh, (x + 1) % 4, c),
        xm=at(yh, (x + 3) % 4, c),
        x2=at(yh, (x + 2) % 4, c),
        yp=at(1 - yh, x, c),
        yxp=at(1 - yh, (x + 1) % 4, c),
        yxm=at(1 - yh, (x + 3) % 4, c),
        yx2=at(1 - yh, (x + 2) % 4, c),
        co=at(yh, x, 1 - c),
        zp={"grp": l * 8 + (z + 1) % 8},
        zm={"grp": l * 8 + (z + 7) % 8},
        lp={"grp": (1 - l) * 8 + z},
    )


def remote(src, dst, send, recv, k, device):
    return pltpu.make_async_remote_copy(
        src_ref=src, dst_ref=dst, send_sem=send.at[k], recv_sem=recv.at[k], device_id=device, device_id_type=MESH
    )


def entry_barrier(devices):
    barrier = pltpu.get_barrier_semaphore()
    for device in devices:
        pl.semaphore_signal(barrier, inc=1, device_id=device, device_id_type=MESH)
    pl.semaphore_wait(barrier, len(devices))


def ring_slot(step, stream, way):
    return 2 + 4 * (step - 1) + 2 * stream + way if step < 4 else 14 + stream


def stacked_heads(both):
    wide = both.astype(F32)
    turned = pltpu.roll(wide, HEAD_DIM, 1)
    low = lax.broadcasted_iota(jnp.int32, wide.shape, 1) < HEAD_DIM
    zero = jnp.zeros_like(wide)
    first0, second0 = jnp.where(low, wide, zero), jnp.where(low, zero, turned)
    first1, second1 = jnp.where(low, turned, zero), jnp.where(low, zero, wide)
    pair = lambda a, b: jnp.concatenate([a, b], axis=0).astype(BF)
    return pair(first0, second0), pair(first0, second1), pair(first1, second1)


def of_pair(p, three):
    return three[0] if p < 3 else three[1] if p == 3 else three[2]


def forward_clients(slot, count, xs_ref, gain, wq_ref, wkv_ref, nt_ref, at_ref, q_ref, kv_ref, pt_ref, att_ref):
    size = count * TOK
    xf = xs_ref[pl.ds(slot, count)].reshape(size, D).astype(F32)
    inv = lax.rsqrt(jnp.mean(xf * xf, axis=-1, keepdims=True) + EPS)
    normed = (xf * inv * gain).astype(BF)
    columns = pl.ds(pl.multiple_of(slot * TOK, TOK), size)
    nt_ref[:, columns] = normed.T
    q_ref[pl.ds(slot, count)] = mm(normed, wq_ref[...]).astype(BF).reshape(count, TOK, D)
    kv = mm(normed, wkv_ref[...]).astype(BF)
    kv_ref[pl.ds(slot, count)] = kv.reshape(count, TOK, 2 * TOK)
    split = [kv[n * TOK : (n + 1) * TOK] for n in range(count)]
    keys = [stacked_heads(s[:, :TOK]) for s in split]
    vals = [stacked_heads(s[:, TOK:]) for s in split]
    s_at = lax.broadcasted_iota(jnp.int32, (TOK, TOK), 0)
    t_at = lax.broadcasted_iota(jnp.int32, (TOK, TOK), 1)
    seen = s_at <= t_at
    for p in range(PAIRS):
        cols = slice(p * TOK, (p + 1) * TOK)
        for n in range(count):
            scores = mm(of_pair(p, keys[n]), q_ref[slot + n, :, cols], NT) * SCALE
            halves = []
            for h in range(2):
                s = jnp.where(seen, scores[h * TOK : (h + 1) * TOK], -1e30)
                e = jnp.exp(s - jnp.max(s, axis=0, keepdims=True))
                halves.append((e * (1.0 / jnp.sum(e, axis=0, keepdims=True))).astype(BF))
            pt = jnp.concatenate(halves, axis=0)
            pt_ref[slot + n, p] = pt
            att_ref[n * TOK : (n + 1) * TOK, cols] = mm(pt, of_pair(p, vals[n]), TN).astype(BF)
    at_ref[:, columns] = att_ref[:size, :].T
    return xf


def backward_clients(slot, count, cg_ref, wo_ref, q_ref, kv_ref, pt_ref, dq_ref, dkv_ref, datt_ref):
    size = count * TOK
    datt_ref[:size, :] = mm(cg_ref[pl.ds(slot, count)].reshape(size, D), wo_ref[...], NT).astype(BF)
    split = [kv_ref[slot + n] for n in range(count)]
    keys = [stacked_heads(s[:, :TOK]) for s in split]
    vals = [stacked_heads(s[:, TOK:]) for s in split]
    sums = {}

    def add(key, value):
        sums[key] = value if key not in sums else sums[key] + value

    for p in range(PAIRS):
        cols = slice(p * TOK, (p + 1) * TOK)
        for n in range(count):
            d_out = datt_ref[n * TOK : (n + 1) * TOK, cols]
            pt = pt_ref[slot + n, p]
            d_probs = mm(of_pair(p, vals[n]), d_out, NT)
            wide = pt.astype(F32)
            halves = []
            for h in range(2):
                half = slice(h * TOK, (h + 1) * TOK)
                both = d_probs[half] * wide[half]
                halves.append((both - wide[half] * jnp.sum(both, axis=0, keepdims=True)) * SCALE)
            ds = jnp.concatenate(halves, axis=0).astype(BF)
            dq_ref[slot + n, :, cols] = mm(ds, of_pair(p, keys[n]), TN).astype(BF)
            dk, dv = mm(ds, q_ref[slot + n, :, cols]), mm(pt, d_out)
            for h in range(2):
                kv_head = (2 * p + h) // PAIRS
                half = slice(h * TOK, (h + 1) * TOK)
                add((n, "k", kv_head, h), dk[half])
                add((n, "v", kv_head, h), dv[half])
    low = lax.broadcasted_iota(jnp.int32, (TOK, TOK), 1) < HEAD_DIM
    for n in range(count):
        for at, name in enumerate(("k", "v")):
            first = sums[n, name, 0, 0] + pltpu.roll(sums[n, name, 0, 1], HEAD_DIM, 1)
            second = sums[n, name, 1, 1] + pltpu.roll(sums[n, name, 1, 0], HEAD_DIM, 1)
            dkv_ref[slot + n, :, at * TOK : (at + 1) * TOK] = jnp.where(low, first, second).astype(BF)


def last_products(left_ref, pairs):
    step = D // 4

    @pl.loop(0, 4)
    def _(t):
        rows = pl.ds(pl.multiple_of(t * step, step), step)
        for right_ref, out_ref in pairs:
            right = right_ref[...].reshape(16 * TOK, right_ref.shape[-1])
            out_ref[rows, :] = (mm(left_ref[rows, :], right) * (1.0 / 16)).astype(BF)


def server_layer(mc_ref, sgain, ws_ref, served_ref, ls_ref, gr_ref, ns_ref, act_ref, sum_ref):
    size = 2 * TOK
    sum_ref[...] = mc_ref[8].astype(F32)

    @pl.loop(0, 4)
    def _(j):
        hf = mc_ref[pl.ds(2 * j, 2)].reshape(size, D).astype(F32)
        cot = mc_ref[pl.ds(8 + 2 * j, 2)].reshape(size, D)
        inv = lax.rsqrt(jnp.mean(hf * hf, axis=-1, keepdims=True) + EPS)
        normed = (hf * inv * sgain).astype(BF)
        ns_ref[pl.ds(pl.multiple_of(j * size, size), size), :] = normed
        gate, up = mm(ws_ref[0], normed, NT), mm(ws_ref[1], normed, NT)
        d_hidden = mm(ws_ref[2], cot, NT)
        sigma = jax.nn.sigmoid(gate)
        silu = gate * sigma
        hidden = (silu * up).astype(BF)
        d_gate = (d_hidden * up * sigma * (1.0 + gate * (1.0 - sigma))).astype(BF)
        d_up = (d_hidden * silu).astype(BF)
        columns = pl.ds(pl.multiple_of(j * size, size), size)
        act_ref[0, :, columns] = d_gate
        act_ref[1, :, columns] = d_up
        act_ref[2, :, columns] = hidden
        served_ref[pl.ds(2 * j, 2)] = mm(hidden, ws_ref[2], TN).astype(BF).reshape(2, TOK, D)
        scaled = (mm(d_gate, ws_ref[0], TN) + mm(d_up, ws_ref[1], TN)) * sgain
        pushed = inv * scaled - hf * (inv * inv * inv) * jnp.mean(scaled * hf, axis=-1, keepdims=True)
        sum_ref[...] += pushed[:TOK] + pushed[TOK:]

    ls_ref[...] = sum_ref[...].reshape(16, 8, D).astype(BF)


def server_gradients(mc_ref, gr_ref, ns_ref, act_ref):
    width = gr_ref.shape[1] // 2

    @pl.loop(0, 2)
    def _(t):
        rows = pl.ds(pl.multiple_of(t * width, 16), width)
        gr_ref[0, rows, :] = mm(act_ref[0, rows, :], ns_ref[...]).astype(BF)
        gr_ref[1, rows, :] = mm(act_ref[1, rows, :], ns_ref[...]).astype(BF)
        gr_ref[2, rows, :] = mm(act_ref[2, rows, :], mc_ref[pl.ds(8, 8)].reshape(8 * TOK, D)).astype(BF)


def step_kernel(
    valid_ref, x_ref, cot_ref, gain_ref, sgain_ref, wq_hbm, wkv_hbm, wo_hbm, wg_hbm, wu_hbm, wd_hbm,
    out_ref, gq_hbm, gkv_hbm, go_hbm, own_hbm, got_hbm,
    wq_ref, wkv_ref, wo_ref, ws_ref, xs_ref, mc_ref, nt_ref, at_ref, q_ref, kv_ref, pt_ref, att_ref,
    served_ref, gr_ref, ns_ref, act_ref, sum_ref, ls_ref, part_ref, mine_ref, slices_ref, cg_ref, back_ref, dkv_ref,
    load, send_m, recv_m, send_x, recv_x, send_w, recv_w, send_r, recv_r, send_a, recv_a,
    send_z, recv_z, send_c, recv_c, send_s, recv_s, send_g, recv_g, keep,
):
    pos = places()
    m, c = pos["m"], pos["c"]
    width = wg_hbm.shape[0]
    near, far = pl.ds(0, width), pl.ds(width, width)
    weights = (wg_hbm, wu_hbm, wd_hbm)
    loads = [
        pltpu.make_async_copy(s, d, load.at[k])
        for k, (s, d) in enumerate(
            [(wq_hbm, wq_ref), (wkv_hbm, wkv_ref), (wo_hbm, wo_ref)]
            + [(w, ws_ref.at[k, near]) for k, w in enumerate(weights)]
        )
    ]
    for copy in loads:
        copy.start()
    live = lax.broadcasted_iota(jnp.int32, (TOK, D), 0) < valid_ref[0, 0]
    mc_ref[8] = jnp.where(live, cot_ref[...].astype(F32), 0.0).astype(BF)
    xs_ref[0] = x_ref[...]

    peers = [{"mem": (m + d) % 16} for d in range(1, 16)]
    entry_barrier(peers + [pos[k] for k in ("zp", "zm", "lp")])
    lo, hi = pl.ds(0, HALF), pl.ds(HALF, HALF)

    def mem_copies(sems, base):
        at = lambda k: mc_ref.at[base + k]
        plan = [
            (at(0), at(1), "xp"),
            (at(0), at(2), "xm"),
            (at(0), at(4), "yp"),
            (mc_ref.at[base + 1, lo], mc_ref.at[base + 3, lo], "xp"),
            (mc_ref.at[base + 2, hi], mc_ref.at[base + 3, hi], "xm"),
            (at(4), at(5), "xp"),
            (at(4), at(6), "xm"),
            (mc_ref.at[base + 5, lo], mc_ref.at[base + 7, lo], "xp"),
            (mc_ref.at[base + 6, hi], mc_ref.at[base + 7, hi], "xm"),
        ]
        return [remote(s, d, send_m, recv_m, sems + k, pos[n]) for k, (s, d, n) in enumerate(plan)]

    cot, cut = mem_copies(0, 8), mem_copies(9, 0)

    def ring_copies(first, block, send, recv):
        ring = {}
        for stream in range(2):
            for way, name in ((0, "zp"), (1, "zm")):
                for step in range(1, 5):
                    before = stream if step == 1 else ring_slot(step - 1, stream, way)
                    after = ring_slot(step, stream, way)
                    src = first if before == 0 else block(before, step == 4, way)
                    k = 1 + (step - 1) * 4 + stream * 2 + way
                    ring[step, stream, way] = remote(src, block(after, step == 4, way), send, recv, k, pos[name])
        return remote(first, block(1, False, 0), send, recv, 0, pos["lp"]), ring

    def input_block(slot, halved, way):
        return xs_ref.at[slot, (lo, hi)[way]] if halved else xs_ref.at[slot]

    in_across, in_ring = ring_copies(x_ref, input_block, send_x, recv_x)
    swap = [remote(w, ws_ref.at[k, far], send_w, recv_w, k, pos["co"]) for k, w in enumerate(weights)]

    def grad_block(slot, halved, way):
        start, size = (way * 32, 32) if halved else (0, HALF)
        return cg_ref.at[slot, pl.ds(pl.multiple_of(c * HALF + start, 32), size)]

    cg_across, cg_ring = ring_copies(grad_block(0, False, 0), grad_block, send_z, recv_z)
    over = {
        slot: remote(grad_block(slot, False, 0), grad_block(slot, False, 0), send_c, recv_c, slot - 1, pos["co"])
        for slot in range(1, 16)
    }
    shares = [remote(ls_ref.at[(m + d) % 16], part_ref.at[d - 1], send_r, recv_r, d - 1, peers[d - 1]) for d in range(1, 16)]
    spread = [remote(mine_ref, slices_ref.at[m], send_a, recv_a, d, peers[d]) for d in range(15)]
    names = ("xm", "xp", "x2", "yp", "yxm", "yxp", "yx2")
    serve = [remote(served_ref.at[k + 1], back_ref.at[k], send_s, recv_s, k, pos[n]) for k, n in enumerate(names)]
    trade = [remote(gr_ref.at[k, far], got_hbm.at[k], send_g, recv_g, k, pos["co"]) for k in range(3)]
    keeps = [pltpu.make_async_copy(gr_ref.at[k, near], own_hbm.at[k], keep.at[k]) for k in range(3)]

    for copy in [in_across] + cot[:3] + [in_ring[1, 0, 0], in_ring[1, 0, 1]] + swap:
        copy.start()
    gain, sgain = gain_ref[...], sgain_ref[...]
    for copy in loads[:3]:
        copy.wait()
    saved = (nt_ref, at_ref, q_ref, kv_ref, pt_ref, att_ref)
    xf = forward_clients(0, 1, xs_ref, gain, wq_ref, wkv_ref, *saved)
    mc_ref[0] = (xf + mm(att_ref[:TOK, :], wo_ref[...])).astype(BF)
    for copy in cut[:3]:
        copy.start()

    def from_neighbours(copies):
        copies[0].wait_recv()
        copies[3].start()
        copies[1].wait_recv()
        copies[4].start()

    def from_across(copies):
        copies[2].wait_recv()
        copies[5].start()
        copies[6].start()

    def from_far(copies):
        copies[5].wait_recv()
        copies[7].start()
        copies[6].wait_recv()
        copies[8].start()

    def inputs(step, stream):
        for way in range(2):
            in_ring[step, stream, way].wait_recv()
            if step < 4:
                in_ring[step + 1, stream, way].start()

    def first_inputs():
        in_across.wait_recv()
        in_ring[1, 1, 0].start()
        in_ring[1, 1, 1].start()

    def server():
        for copies in (cot, cut):
            for k in (3, 4, 7, 8):
                copies[k].wait_recv()
        for copy in loads[3:]:
            copy.wait()
        for copy in swap:
            copy.wait_recv()
        server_layer(mc_ref, sgain, ws_ref, served_ref, ls_ref, gr_ref, ns_ref, act_ref, sum_ref)
        for copy in shares:
            copy.start()

    def gradients():
        server_gradients(mc_ref, gr_ref, ns_ref, act_ref)
        sum_ref[...] = mc_ref[0].astype(F32)

    def reduce():
        total = ls_ref[m].astype(F32)
        for d in range(15):
            shares[d].wait_recv()
            total = total + part_ref[d].astype(F32)
        mine_ref[...] = (total * (1.0 / 16)).astype(BF)
        for copy in spread:
            copy.start()
        slices_ref[m] = mine_ref[...]

    def own_group():
        for d in range(15):
            spread[d].wait_recv()
        cg_ref[0] = slices_ref[...].astype(F32).reshape(TOK, D).astype(BF)
        for copy in [cg_across, cg_ring[1, 0, 0], cg_ring[1, 0, 1]] + serve + trade + keeps:
            copy.start()

    def when_at(i, events):
        for at, todo in events.items():
            @pl.when(i == at)
            def _():
                for act in todo:
                    act()

    forward_events = {
        0: [first_inputs, lambda: from_neighbours(cot), lambda: from_across(cot)],
        1: [lambda: inputs(1, 0), lambda: from_neighbours(cut), lambda: from_across(cut)],
        2: [lambda: inputs(1, 1), lambda: from_far(cot)],
        3: [lambda: inputs(2, 0), lambda: from_far(cut)],
        4: [lambda: inputs(2, 1)],
        5: [server, lambda: inputs(3, 0), gradients],
        6: [reduce, lambda: inputs(3, 1)],
        7: [lambda: inputs(4, 0), lambda: inputs(4, 1), own_group],
    }

    @pl.loop(0, 8)
    def _(j):
        when_at(j, forward_events)
        forward_clients(2 * j, 2, xs_ref, gain, wq_ref, wkv_ref, *saved)

    def grads(step, stream):
        for way in range(2):
            cg_ring[step, stream, way].wait_recv()
            if step < 4:
                cg_ring[step + 1, stream, way].start()
                over[ring_slot(step, stream, way)].start()
        if step == 4:
            over[14 + stream].start()

    def first_grads():
        cg_across.wait_recv()
        cg_ring[1, 1, 0].start()
        cg_ring[1, 1, 1].start()
        over[1].start()

    def handed(*slots):
        for slot in slots:
            over[slot].wait_recv()

    for copy in cot + cut:
        copy.wait_send()
    backward_events = {
        0: [first_grads, lambda: grads(1, 0), lambda: handed(1)],
        1: [lambda: grads(1, 1), lambda: handed(2, 3)],
        2: [lambda: grads(2, 0), lambda: handed(4, 5)],
        3: [lambda: grads(2, 1), lambda: handed(6, 7)],
        4: [lambda: grads(3, 0), lambda: handed(8, 9)],
        5: [lambda: grads(3, 1), lambda: handed(10, 11)],
        6: [lambda: grads(4, 0), lambda: grads(4, 1), lambda: handed(12, 13)],
        7: [lambda: handed(14, 15)],
    }

    @pl.loop(0, 8)
    def _(j):
        when_at(j, backward_events)
        backward_clients(2 * j, 2, cg_ref, wo_ref, q_ref, kv_ref, pt_ref, mc_ref, dkv_ref, att_ref)

    go_ref = ns_ref.at[pl.ds(0, D)]
    done = [
        pltpu.make_async_copy(s, d, load.at[k])
        for k, (s, d) in enumerate([(go_ref, go_hbm), (wq_ref, gq_hbm), (wkv_ref, gkv_hbm)])
    ]
    last_products(at_ref, [(cg_ref, go_ref)])
    done[0].start()
    last_products(nt_ref, [(mc_ref, wq_ref), (dkv_ref, wkv_ref)])
    done[1].start()
    done[2].start()

    for copy in serve:
        copy.wait_recv()
    out = sum_ref[...] + served_ref[0].astype(F32)
    for k in range(7):
        out = out + back_ref[k].astype(F32)
    out_ref[...] = out.astype(BF)
    for copy in trade:
        copy.wait_recv()
    for copy in keeps + done:
        copy.wait()
    for copy in [in_across, cg_across] + list(in_ring.values()) + list(cg_ring.values()) + list(over.values()):
        copy.wait_send()
    for copy in swap + shares + spread + serve + trade:
        copy.wait_send()


def step_call(valid, x, cot, gain, sgain, wq, wkv, wo, wg, wu, wd):
    vmem, anyspace = pl.BlockSpec(memory_space=pltpu.VMEM), pl.BlockSpec(memory_space=pl.ANY)
    sds = jax.ShapeDtypeStruct
    sem = pltpu.SemaphoreType.DMA
    width = wg.shape[0]
    units = 2 * width
    block = pltpu.VMEM((TOK, D), BF)
    blocks = lambda n: pltpu.VMEM((n, TOK, D), BF)
    return pl.pallas_call(
        step_kernel,
        out_shape=(
            sds((TOK, D), BF), sds((D, D), BF), sds((D, 2 * TOK), BF), sds((D, D), BF),
            sds((3, width, D), BF), sds((3, width, D), BF),
        ),
        in_specs=[pl.BlockSpec(memory_space=pltpu.SMEM)] + [vmem] * 4 + [anyspace] * 6,
        out_specs=[vmem] + [anyspace] * 5,
        scratch_shapes=[
            pltpu.VMEM((D, D), BF), pltpu.VMEM((D, 2 * TOK), BF), pltpu.VMEM((D, D), BF), pltpu.VMEM((3, units, D), BF),
            blocks(16), blocks(16), pltpu.VMEM((D, 16 * TOK), BF), pltpu.VMEM((D, 16 * TOK), BF),
            blocks(16), pltpu.VMEM((16, TOK, 2 * TOK), BF), pltpu.VMEM((16, PAIRS, 2 * TOK, TOK), BF),
            pltpu.VMEM((2 * TOK, D), BF),
            blocks(8), pltpu.VMEM((3, units, D), BF), pltpu.VMEM((8 * TOK, D), BF), pltpu.VMEM((3, units, 8 * TOK), BF),
            pltpu.VMEM((TOK, D), F32), pltpu.VMEM((16, 8, D), BF), pltpu.VMEM((15, 8, D), BF), pltpu.VMEM((8, D), BF),
            pltpu.VMEM((16, 8, D), BF), blocks(16), blocks(7), pltpu.VMEM((16, TOK, 2 * TOK), BF),
            sem((6,)), sem((18,)), sem((18,)), sem((17,)), sem((17,)), sem((3,)), sem((3,)), sem((15,)), sem((15,)),
            sem((15,)), sem((15,)), sem((17,)), sem((17,)), sem((15,)), sem((15,)), sem((7,)), sem((7,)),
            sem((3,)), sem((3,)), sem((3,)),
        ],
        compiler_params=pltpu.CompilerParams(collective_id=0, has_side_effects=True, vmem_limit_bytes=60 * 1024 * 2**10),
        name="split_step",
    )(valid, x, cot, gain, sgain, wq, wkv, wo, wg, wu, wd)


def on_device(
    client_input, client_gain, w_query, w_keyval, w_out, server_gain, w_gate, w_up, w_down, out_grad, valid
):
    server_out, grad_q, grad_kv, grad_o, own, got = step_call(
        valid, client_input[0, 0], out_grad[0, 0], client_gain, server_gain, w_query[0], w_keyval[0], w_out[0],
        w_gate[0].T, w_up[0].T, w_down[0],
    )
    joined = (own.astype(F32) + got.astype(F32)).astype(BF)
    return (
        server_out[None, None],
        grad_q[None],
        grad_kv[None],
        grad_o[None],
        joined[0].T[None],
        joined[1].T[None],
        joined[2][None],
    )


def solution(mesh):
    in_specs = (
        P("grp", "mem", None, None),
        P("mem", None),
        P("mem", None, None),
        P("mem", None, None),
        P("mem", None, None),
        P("grp", None),
        P("grp", None, "mem"),
        P("grp", None, "mem"),
        P("grp", "mem", None),
        P("grp", "mem", None, None),
        P("grp", "mem"),
    )
    out_specs = (
        P("grp", "mem", None, None),
        P("mem", None, None),
        P("mem", None, None),
        P("mem", None, None),
        P("grp", None, "mem"),
        P("grp", None, "mem"),
        P("grp", "mem", None),
    )
    return jax.shard_map(
        on_device, mesh=mesh, in_specs=in_specs, out_specs=out_specs, check_vma=False
    )
```

time: 435 us -> 130 us (0.30); the launches traced: 427 us -> 130 us
  waiting for transfers between devices: 333 us -> 0 us
  Pallas kernels: 0 us -> 121 us
  matrix products: 42.4 us -> 0 us
  other arithmetic: 30.3 us -> 2.32 us
  between operations: 15 us -> 1.32 us
    psum x1 -> x0, waiting for transfers between devices: 144 us -> none  [on_device(): lax.psum(grad_q.astype(jnp.float32).astype(jnp.bfloat16), 'grp')]
    all_gather x2 -> x0, waiting for transfers between devices: 128 us -> none  [the longest x1 77.5 us: side_by_side(): filled = lax.all_gather(both, axis, axis=dim, tiled=True)]
    pallas_call x0 -> x1, Pallas kernels: none -> 121 us  [step_call(): pl.pallas_call(step_kernel, out_shape=(sds((TOK, D), BF), sds((D, D), BF)...]
    reduce_scatter x1 -> x0, waiting for transfers between devices: 60.4 us -> none  [on_device(): lax.psum_scatter(jnp.dot(hidden, down_w, preferred_element_type=jnp.float...]
    dot_general x22 -> x0, matrix products: 42.4 us -> none  [the longest x1 5.6 us: on_device(): jnp.dot(hidden, down_w, preferred_element_type=jnp.float32)]
    reduce_sum x6 -> x0, other arithmetic: 11.3 us -> none  [the longest x1 4.23 us: on_device(): jnp.sum(pushed.reshape(-1, length, width), axis=0)]
    broadcast_in_dim x3 -> x0, other arithmetic: 7.73 us -> none  [the longest x1 4.18 us: on_device(): grad_query[None]]
  transfers between devices with their start and end apart: 4 -> 0, of which waited for: 4 -> 0; matrix products, arithmetic and copies ran while one was open for 8% -> 0% of each run, Pallas kernels for 0% -> 0%
where the time goes in v2:
time: 130 us
  Pallas kernels  121 us (93%)
  local copies, waits for them, and re-layouts  5.43 us (4%)
  other arithmetic  2.32 us (2%)
  between operations  1.32 us (1%)
    pallas_call x1, Pallas kernels, step_call(): pl.pallas_call(step_kernel, out_shape=(sds((TOK, D), BF), sds((D, D), BF)...  121 us
    unnamed x12, local copies, waits for them, and re-layouts  4.23 us

profile of v2, /device:TPU:1, one launch (start us, length us, event | category | flops | bytes accessed | tf_op | source)
XLA Modules:
  0.0 129.7 jit_solution(15364885334422093059)
XLA Ops:
  1.3 120.6 %split_step.1 = (bf16[128,896]{1,0:T(8,128)(2,1)}, bf16[896,896]{1,0:T(8,128)(2,1)}, bf16[896,256]{1,0:T(8,128)(2,1)}, bf16[896,896]{1,0:T(8,128)(2,1)}, bf16[3,...) custom-call(s32[1,1]{1,0:T(1,128)S(6)} %copy.22.valid_ref, bf16[128,896]{1,0:T(8,128)(2,1)} %bitcast.38, ...), custom_call_target="tpu_custom_call" | custom-call | tf_op jit(solution)/shard_map/split_step/pallas_call | solution.py:454
  121.9 2.3 %add_convert_fusion = bf16[3,304,896]{2,1,0:T(8,128)(2,1)S(1)} fusion(bf16[3,304,896]{2,1,0:T(8,128)(2,1)} %get-tuple-element.18, bf16[3,304,896]{2,1,0:T(8,128)(2,1)} %get-tuple-element.17), kind=kLoop, calls=%fused_computation | loop fusion | flops 3268608 | bytes 4902912 | tf_op jit(solution)/shard_map/convert_element_type | solution.py:486
  124.2 0.0 copy-start.3
  124.2 0.0 copy-start.1
  124.2 1.2 fusion
  125.4 0.0 copy-done.3
  125.4 0.7 copy.23
  126.1 0.2 copy-done.1
  126.4 0.0 copy-start.2
  126.4 0.0 copy-start
  126.4 1.2 copy.24
  127.5 0.1 copy-done.2
  127.7 0.8 copy.25
  128.4 0.1 copy-done
  128.5 1.2 copy.26
Async XLA Ops:
  124.2 1.2 copy-start.3
  124.2 2.1 %copy-start.1 = (bf16[896,896]{1,0:T(8,128)(2,1)S(1)}, bf16[896,896]{1,0:T(8,128)(2,1)}, u32[]{:S(2)}) copy-start(bf16[896,896]{1,0:T(8,128)(2,1)} %get-tuple-element.14) | copy-start | bytes 4816900
  126.4 1.3 %copy-start.2 = (bf16[896,256]{1,0:T(8,128)(2,1)S(1)}, bf16[896,256]{1,0:T(8,128)(2,1)}, u32[]{:S(2)}) copy-start(bf16[896,256]{1,0:T(8,128)(2,1)} %get-tuple-element.15) | copy-start | bytes 1376260
  126.4 2.1 %copy-start = (bf16[896,896]{1,0:T(8,128)(2,1)S(1)}, bf16[896,896]{1,0:T(8,128)(2,1)}, u32[]{:S(2)}) copy-start(bf16[896,896]{1,0:T(8,128)(2,1)} %get-tuple-element.16) | copy-start | bytes 4816900

commit v3 on v2

--- a/solution.py
+++ b/solution.py
@@ -65,96 +65,115 @@
     return 2 + 4 * (step - 1) + 2 * stream + way if step < 4 else 14 + stream
 
 
-def stacked_heads(both):
+MEETS = (((0, 4), (4, 7)), ((0, 3), (3, 7)))
+GROUPS = ((0, 3), (3, 4), (4, 7))
+
+
+def head_rows(both):
     wide = both.astype(F32)
     turned = pltpu.roll(wide, HEAD_DIM, 1)
     low = lax.broadcasted_iota(jnp.int32, wide.shape, 1) < HEAD_DIM
     zero = jnp.zeros_like(wide)
-    first0, second0 = jnp.where(low, wide, zero), jnp.where(low, zero, turned)
-    first1, second1 = jnp.where(low, turned, zero), jnp.where(low, zero, wide)
-    pair = lambda a, b: jnp.concatenate([a, b], axis=0).astype(BF)
-    return pair(first0, second0), pair(first0, second1), pair(first1, second1)
-
-
-def of_pair(p, three):
-    return three[0] if p < 3 else three[1] if p == 3 else three[2]
-
-
-def forward_clients(slot, count, xs_ref, gain, wq_ref, wkv_ref, nt_ref, at_ref, q_ref, kv_ref, pt_ref, att_ref):
+    first = (jnp.where(low, wide, zero).astype(BF), jnp.where(low, turned, zero).astype(BF))
+    second = (jnp.where(low, zero, turned).astype(BF), jnp.where(low, zero, wide).astype(BF))
+    return first, second
+
+
+def head_columns(both):
+    turned = both.T
+    zero = jnp.zeros((HEAD_DIM, TOK), BF)
+    heads = (turned[:HEAD_DIM], turned[HEAD_DIM:])
+    build = lambda a, b: jnp.concatenate(
+        [jnp.concatenate([heads[a], zero], axis=1), jnp.concatenate([zero, heads[b]], axis=1)], axis=0
+    )
+    return build(0, 0), build(0, 1), build(1, 1)
+
+
+def lanes(span):
+    return slice(span[0] * TOK, span[1] * TOK)
+
+
+def stack(ref, n, span):
+    return ref[n, span[0] : span[1]].reshape((span[1] - span[0]) * TOK, TOK)
+
+
+def forward_clients(slot, count, xs_ref, gain, wq_ref, wkv_ref, nt_ref, at_ref, q_ref, kv_ref, pt_ref):
     size = count * TOK
     xf = xs_ref[pl.ds(slot, count)].reshape(size, D).astype(F32)
     inv = lax.rsqrt(jnp.mean(xf * xf, axis=-1, keepdims=True) + EPS)
     normed = (xf * inv * gain).astype(BF)
     columns = pl.ds(pl.multiple_of(slot * TOK, TOK), size)
     nt_ref[:, columns] = normed.T
-    q_ref[pl.ds(slot, count)] = mm(normed, wq_ref[...]).astype(BF).reshape(count, TOK, D)
+    queries = mm(normed, wq_ref[...]).astype(BF)
     kv = mm(normed, wkv_ref[...]).astype(BF)
     kv_ref[pl.ds(slot, count)] = kv.reshape(count, TOK, 2 * TOK)
-    split = [kv[n * TOK : (n + 1) * TOK] for n in range(count)]
-    keys = [stacked_heads(s[:, :TOK]) for s in split]
-    vals = [stacked_heads(s[:, TOK:]) for s in split]
+    for n in range(count):
+        for p in range(PAIRS):
+            q_ref[slot + n, p] = queries[n * TOK : (n + 1) * TOK, lanes((p, p + 1))]
     s_at = lax.broadcasted_iota(jnp.int32, (TOK, TOK), 0)
     t_at = lax.broadcasted_iota(jnp.int32, (TOK, TOK), 1)
     seen = s_at <= t_at
-    for p in range(PAIRS):
-        cols = slice(p * TOK, (p + 1) * TOK)
-        for n in range(count):
-            scores = mm(of_pair(p, keys[n]), q_ref[slot + n, :, cols], NT) * SCALE
-            halves = []
-            for h in range(2):
-                s = jnp.where(seen, scores[h * TOK : (h + 1) * TOK], -1e30)
-                e = jnp.exp(s - jnp.max(s, axis=0, keepdims=True))
-                halves.append((e * (1.0 / jnp.sum(e, axis=0, keepdims=True))).astype(BF))
-            pt = jnp.concatenate(halves, axis=0)
-            pt_ref[slot + n, p] = pt
-            att_ref[n * TOK : (n + 1) * TOK, cols] = mm(pt, of_pair(p, vals[n]), TN).astype(BF)
-    at_ref[:, columns] = att_ref[:size, :].T
+    for place in range(2):
+        for head in range(2):
+            span = MEETS[place][head]
+            for n in range(count):
+                keys = head_rows(kv[n * TOK : (n + 1) * TOK, :TOK])
+                scores = mm(keys[place][head], stack(q_ref, slot + n, span), NT) * SCALE
+                for p in range(*span):
+                    s = jnp.where(seen, scores[:, lanes((p - span[0], p - span[0] + 1))], -1e30)
+                    e = jnp.exp(s - jnp.max(s, axis=0, keepdims=True))
+                    pt = (e * (1.0 / jnp.sum(e, axis=0, keepdims=True))).astype(BF)
+                    pt_ref[slot + n, place * TOK : (place + 1) * TOK, lanes((p, p + 1))] = pt
+    for n in range(count):
+        vals = head_columns(kv[n * TOK : (n + 1) * TOK, TOK:])
+        tokens = pl.ds(pl.multiple_of((slot + n) * TOK, TOK), TOK)
+        for span, part in zip(GROUPS, vals):
+            out = mm(part, pt_ref[slot + n, :, lanes(span)]).astype(BF)
+            for p in range(*span):
+                at_ref[lanes((p, p + 1)), tokens] = out[:, lanes((p - span[0], p - span[0] + 1))]
     return xf
 
 
-def backward_clients(slot, count, cg_ref, wo_ref, q_ref, kv_ref, pt_ref, dq_ref, dkv_ref, datt_ref):
+def backward_clients(slot, count, cg_ref, wo_ref, q_ref, kv_ref, pt_ref, dq_ref, dkv_ref, datt_ref, ds_ref):
     size = count * TOK
-    datt_ref[:size, :] = mm(cg_ref[pl.ds(slot, count)].reshape(size, D), wo_ref[...], NT).astype(BF)
-    split = [kv_ref[slot + n] for n in range(count)]
-    keys = [stacked_heads(s[:, :TOK]) for s in split]
-    vals = [stacked_heads(s[:, TOK:]) for s in split]
-    sums = {}
-
-    def add(key, value):
-        sums[key] = value if key not in sums else sums[key] + value
-
-    for p in range(PAIRS):
-        cols = slice(p * TOK, (p + 1) * TOK)
-        for n in range(count):
-            d_out = datt_ref[n * TOK : (n + 1) * TOK, cols]
-            pt = pt_ref[slot + n, p]
-            d_probs = mm(of_pair(p, vals[n]), d_out, NT)
-            wide = pt.astype(F32)
-            halves = []
-            for h in range(2):
-                half = slice(h * TOK, (h + 1) * TOK)
-                both = d_probs[half] * wide[half]
-                halves.append((both - wide[half] * jnp.sum(both, axis=0, keepdims=True)) * SCALE)
-            ds = jnp.concatenate(halves, axis=0).astype(BF)
-            dq_ref[slot + n, :, cols] = mm(ds, of_pair(p, keys[n]), TN).astype(BF)
-            dk, dv = mm(ds, q_ref[slot + n, :, cols]), mm(pt, d_out)
-            for h in range(2):
-                kv_head = (2 * p + h) // PAIRS
-                half = slice(h * TOK, (h + 1) * TOK)
-                add((n, "k", kv_head, h), dk[half])
-                add((n, "v", kv_head, h), dv[half])
+    datt = mm(cg_ref[pl.ds(slot, count)].reshape(size, D), wo_ref[...], NT).astype(BF)
+    for n in range(count):
+        for p in range(PAIRS):
+            datt_ref[n, p] = datt[n * TOK : (n + 1) * TOK, lanes((p, p + 1))]
+    for place in range(2):
+        keys_at = slice(place * TOK, (place + 1) * TOK)
+        for head in range(2):
+            span = MEETS[place][head]
+            for n in range(count):
+                vals = head_rows(kv_ref[slot + n, :, TOK:])
+                d_probs = mm(vals[place][head], stack(datt_ref, n, span), NT)
+                for p in range(*span):
+                    wide = pt_ref[slot + n, keys_at, lanes((p, p + 1))].astype(F32)
+                    both = d_probs[:, lanes((p - span[0], p - span[0] + 1))] * wide
+                    ds = (both - wide * jnp.sum(both, axis=0, keepdims=True)) * SCALE
+                    ds_ref[n, keys_at, lanes((p, p + 1))] = ds.astype(BF)
     low = lax.broadcasted_iota(jnp.int32, (TOK, TOK), 1) < HEAD_DIM
     for n in range(count):
-        for at, name in enumerate(("k", "v")):
-            first = sums[n, name, 0, 0] + pltpu.roll(sums[n, name, 0, 1], HEAD_DIM, 1)
-            second = sums[n, name, 1, 1] + pltpu.roll(sums[n, name, 1, 0], HEAD_DIM, 1)
-            dkv_ref[slot + n, :, at * TOK : (at + 1) * TOK] = jnp.where(low, first, second).astype(BF)
+        keys = head_columns(kv_ref[slot + n, :, :TOK])
+        for span, part in zip(GROUPS, keys):
+            out = mm(part, ds_ref[n, :, lanes(span)]).astype(BF)
+            for p in range(*span):
+                dq_ref[slot + n, :, lanes((p, p + 1))] = out[:, lanes((p - span[0], p - span[0] + 1))].T
+        for at in range(2):
+            left = (lambda k, l: ds_ref[n, k, l]) if at == 0 else (lambda k, l: pt_ref[slot + n, k, l])
+            right = (lambda span: stack(q_ref, slot + n, span)) if at == 0 else (lambda span: stack(datt_ref, n, span))
+            total = [
+                [mm(left(slice(o * TOK, (o + 1) * TOK), lanes(span)), right(span)) for span in MEETS[o]] for o in range(2)
+            ]
+            first = total[0][0] + pltpu.roll(total[1][0], HEAD_DIM, 1)
+            second = total[1][1] + pltpu.roll(total[0][1], HEAD_DIM, 1)
+            dkv_ref[slot + n, :, lanes((at, at + 1))] = jnp.where(low, first, second).astype(BF)
 
 
 def last_products(left_ref, pairs):
-    step = D // 4
-
-    @pl.loop(0, 4)
+    step = D // 2
+
+    @pl.loop(0, 2)
     def _(t):
         rows = pl.ds(pl.multiple_of(t * step, step), step)
         for right_ref, out_ref in pairs:
@@ -162,34 +181,29 @@
             out_ref[rows, :] = (mm(left_ref[rows, :], right) * (1.0 / 16)).astype(BF)
 
 
-def server_layer(mc_ref, sgain, ws_ref, served_ref, ls_ref, gr_ref, ns_ref, act_ref, sum_ref):
+def server_rows(j, mc_ref, sgain, ws_ref, served_ref, ns_ref, act_ref, sum_ref):
     size = 2 * TOK
-    sum_ref[...] = mc_ref[8].astype(F32)
-
-    @pl.loop(0, 4)
-    def _(j):
-        hf = mc_ref[pl.ds(2 * j, 2)].reshape(size, D).astype(F32)
-        cot = mc_ref[pl.ds(8 + 2 * j, 2)].reshape(size, D)
-        inv = lax.rsqrt(jnp.mean(hf * hf, axis=-1, keepdims=True) + EPS)
-        normed = (hf * inv * sgain).astype(BF)
-        ns_ref[pl.ds(pl.multiple_of(j * size, size), size), :] = normed
-        gate, up = mm(ws_ref[0], normed, NT), mm(ws_ref[1], normed, NT)
-        d_hidden = mm(ws_ref[2], cot, NT)
-        sigma = jax.nn.sigmoid(gate)
-        silu = gate * sigma
-        hidden = (silu * up).astype(BF)
-        d_gate = (d_hidden * up * sigma * (1.0 + gate * (1.0 - sigma))).astype(BF)
-        d_up = (d_hidden * silu).astype(BF)
-        columns = pl.ds(pl.multiple_of(j * size, size), size)
-        act_ref[0, :, columns] = d_gate
-        act_ref[1, :, columns] = d_up
-        act_ref[2, :, columns] = hidden
-        served_ref[pl.ds(2 * j, 2)] = mm(hidden, ws_ref[2], TN).astype(BF).reshape(2, TOK, D)
-        scaled = (mm(d_gate, ws_ref[0], TN) + mm(d_up, ws_ref[1], TN)) * sgain
-        pushed = inv * scaled - hf * (inv * inv * inv) * jnp.mean(scaled * hf, axis=-1, keepdims=True)
-        sum_ref[...] += pushed[:TOK] + pushed[TOK:]
-
-    ls_ref[...] = sum_ref[...].reshape(16, 8, D).astype(BF)
+    units = ws_ref.shape[1]
+    hf = mc_ref[pl.ds(2 * j, 2)].reshape(size, D).astype(F32)
+    cot = mc_ref[pl.ds(8 + 2 * j, 2)].reshape(size, D)
+    inv = lax.rsqrt(jnp.mean(hf * hf, axis=-1, keepdims=True) + EPS)
+    normed = (hf * inv * sgain).astype(BF)
+    columns = pl.ds(pl.multiple_of(j * size, size), size)
+    ns_ref[columns, :] = normed
+    gate, up = mm(ws_ref[0], normed, NT), mm(ws_ref[1], normed, NT)
+    d_hidden = mm(ws_ref[2], cot, NT)
+    sigma = jax.nn.sigmoid(gate)
+    silu = gate * sigma
+    act_ref[2, :, columns] = (silu * up).astype(BF)
+    act_ref[0, :, columns] = (d_hidden * up * sigma * (1.0 + gate * (1.0 - sigma))).astype(BF)
+    act_ref[1, :, columns] = (d_hidden * silu).astype(BF)
+    served = mm(act_ref[2, :, columns], ws_ref[2], TN).astype(BF)
+    served_ref[pl.ds(2 * j, 2)] = served.reshape(2, TOK, D)
+    both = act_ref[pl.ds(0, 2), :, columns].reshape(2 * units, size)
+    scaled = mm(both, ws_ref[pl.ds(0, 2)].reshape(2 * units, D), TN) * sgain
+    hf = mc_ref[pl.ds(2 * j, 2)].reshape(size, D).astype(F32)
+    pushed = inv * scaled - hf * (inv * inv * inv) * jnp.mean(scaled * hf, axis=-1, keepdims=True)
+    sum_ref[...] += pushed[:TOK] + pushed[TOK:]
 
 
 def server_gradients(mc_ref, gr_ref, ns_ref, act_ref):
@@ -205,8 +219,8 @@
 
 def step_kernel(
     valid_ref, x_ref, cot_ref, gain_ref, sgain_ref, wq_hbm, wkv_hbm, wo_hbm, wg_hbm, wu_hbm, wd_hbm,
-    out_ref, gq_hbm, gkv_hbm, go_hbm, own_hbm, got_hbm,
-    wq_ref, wkv_ref, wo_ref, ws_ref, xs_ref, mc_ref, nt_ref, at_ref, q_ref, kv_ref, pt_ref, att_ref,
+    out_ref, gq_hbm, gkv_hbm, go_hbm, own_g, own_u, own_d, got_g, got_u, got_d,
+    wq_ref, wkv_ref, wo_ref, ws_ref, xs_ref, mc_ref, nt_ref, at_ref, q_ref, kv_ref, pt_ref, datt_ref, ds_ref,
     served_ref, gr_ref, ns_ref, act_ref, sum_ref, ls_ref, part_ref, mine_ref, slices_ref, cg_ref, back_ref, dkv_ref,
     load, send_m, recv_m, send_x, recv_x, send_w, recv_w, send_r, recv_r, send_a, recv_a,
     send_z, recv_z, send_c, recv_c, send_s, recv_s, send_g, recv_g, keep,
@@ -238,17 +252,16 @@
         plan = [
             (at(0), at(1), "xp"),
             (at(0), at(2), "xm"),
-            (at(0), at(4), "yp"),
-            (mc_ref.at[base + 1, lo], mc_ref.at[base + 3, lo], "xp"),
-            (mc_ref.at[base + 2, hi], mc_ref.at[base + 3, hi], "xm"),
-            (at(4), at(5), "xp"),
-            (at(4), at(6), "xm"),
-            (mc_ref.at[base + 5, lo], mc_ref.at[base + 7, lo], "xp"),
-            (mc_ref.at[base + 6, hi], mc_ref.at[base + 7, hi], "xm"),
+            (at(0), at(3), "yp"),
+            (mc_ref.at[base + 1, lo], mc_ref.at[base + 6, lo], "xp"),
+            (mc_ref.at[base + 2, hi], mc_ref.at[base + 6, hi], "xm"),
+            (at(3), at(4), "xp"),
+            (at(3), at(5), "xm"),
+            (at(6), at(7), "yp"),
         ]
         return [remote(s, d, send_m, recv_m, sems + k, pos[n]) for k, (s, d, n) in enumerate(plan)]
 
-    cot, cut = mem_copies(0, 8), mem_copies(9, 0)
+    cot, cut = mem_copies(0, 8), mem_copies(8, 0)
 
     def ring_copies(first, block, send, recv):
         ring = {}
@@ -279,19 +292,22 @@
     }
     shares = [remote(ls_ref.at[(m + d) % 16], part_ref.at[d - 1], send_r, recv_r, d - 1, peers[d - 1]) for d in range(1, 16)]
     spread = [remote(mine_ref, slices_ref.at[m], send_a, recv_a, d, peers[d]) for d in range(15)]
-    names = ("xm", "xp", "x2", "yp", "yxm", "yxp", "yx2")
+    names = ("xm", "xp", "yp", "yxm", "yxp", "x2", "yx2")
     serve = [remote(served_ref.at[k + 1], back_ref.at[k], send_s, recv_s, k, pos[n]) for k, n in enumerate(names)]
-    trade = [remote(gr_ref.at[k, far], got_hbm.at[k], send_g, recv_g, k, pos["co"]) for k in range(3)]
-    keeps = [pltpu.make_async_copy(gr_ref.at[k, near], own_hbm.at[k], keep.at[k]) for k in range(3)]
-
-    for copy in [in_across] + cot[:3] + [in_ring[1, 0, 0], in_ring[1, 0, 1]] + swap:
+    trade = [
+        remote(gr_ref.at[k, far], got, send_g, recv_g, k, pos["co"]) for k, got in enumerate((got_g, got_u, got_d))
+    ]
+    keeps = [pltpu.make_async_copy(gr_ref.at[k, near], own, keep.at[k]) for k, own in enumerate((own_g, own_u, own_d))]
+
+    for copy in [in_ring[1, 0, 0], in_ring[1, 0, 1]] + cot[:2] + [in_across, cot[2]] + swap:
         copy.start()
+    sum_ref[...] = mc_ref[8].astype(F32)
     gain, sgain = gain_ref[...], sgain_ref[...]
     for copy in loads[:3]:
         copy.wait()
-    saved = (nt_ref, at_ref, q_ref, kv_ref, pt_ref, att_ref)
+    saved = (nt_ref, at_ref, q_ref, kv_ref, pt_ref)
     xf = forward_clients(0, 1, xs_ref, gain, wq_ref, wkv_ref, *saved)
-    mc_ref[0] = (xf + mm(att_ref[:TOK, :], wo_ref[...])).astype(BF)
+    mc_ref[0] = (xf + mm(at_ref[:, :TOK], wo_ref[...], TN)).astype(BF)
     for copy in cut[:3]:
         copy.start()
 
@@ -307,10 +323,9 @@
         copies[6].start()
 
     def from_far(copies):
-        copies[5].wait_recv()
+        copies[3].wait_recv()
+        copies[4].wait_recv()
         copies[7].start()
-        copies[6].wait_recv()
-        copies[8].start()
 
     def inputs(step, stream):
         for way in range(2):
@@ -323,15 +338,19 @@
         in_ring[1, 1, 0].start()
         in_ring[1, 1, 1].start()
 
-    def server():
-        for copies in (cot, cut):
-            for k in (3, 4, 7, 8):
-                copies[k].wait_recv()
+    def server_weights():
         for copy in loads[3:]:
             copy.wait()
         for copy in swap:
             copy.wait_recv()
-        server_layer(mc_ref, sgain, ws_ref, served_ref, ls_ref, gr_ref, ns_ref, act_ref, sum_ref)
+
+    def arrived(*which):
+        for copies in (cot, cut):
+            for k in which:
+                copies[k].wait_recv()
+
+    def share():
+        ls_ref[...] = sum_ref[...].reshape(16, 8, D).astype(BF)
         for copy in shares:
             copy.start()
 
@@ -363,21 +382,34 @@
                 for act in todo:
                     act()
 
-    forward_events = {
-        0: [first_inputs, lambda: from_neighbours(cot), lambda: from_across(cot)],
-        1: [lambda: inputs(1, 0), lambda: from_neighbours(cut), lambda: from_across(cut)],
-        2: [lambda: inputs(1, 1), lambda: from_far(cot)],
-        3: [lambda: inputs(2, 0), lambda: from_far(cut)],
+    before_rows = {
+        0: [lambda: from_neighbours(cot), lambda: inputs(1, 0), first_inputs],
+        1: [server_weights, lambda: from_across(cot), lambda: from_neighbours(cut)],
+        2: [lambda: from_across(cut), lambda: from_far(cot)],
+        4: [lambda: inputs(3, 0), lambda: arrived(5, 6)],
+        5: [lambda: arrived(7)],
+        6: [lambda: inputs(3, 1), own_group],
+        7: [lambda: inputs(4, 0), lambda: inputs(4, 1)],
+    }
+    before_pair = {
+        1: [lambda: inputs(2, 0)],
+        2: [lambda: inputs(1, 1), lambda: from_far(cut)],
         4: [lambda: inputs(2, 1)],
-        5: [server, lambda: inputs(3, 0), gradients],
-        6: [reduce, lambda: inputs(3, 1)],
-        7: [lambda: inputs(4, 0), lambda: inputs(4, 1), own_group],
+        5: [share, gradients, reduce],
     }
+    order = sum(pair << (3 * k) for k, pair in enumerate((1, 3, 0, 2, 5, 4, 6, 7)))
 
     @pl.loop(0, 8)
-    def _(j):
-        when_at(j, forward_events)
-        forward_clients(2 * j, 2, xs_ref, gain, wq_ref, wkv_ref, *saved)
+    def _(k):
+        when_at(k, before_rows)
+
+        @pl.when((k % 3 != 0) & (k < 6))
+        def _():
+            server_rows(k - 1 - k // 4, mc_ref, sgain, ws_ref, served_ref, ns_ref, act_ref, sum_ref)
+
+        when_at(k, before_pair)
+        pair = jnp.right_shift(order, 3 * k) % 8
+        forward_clients(2 * pair, 2, xs_ref, gain, wq_ref, wkv_ref, *saved)
 
     def grads(step, stream):
         for way in range(2):
@@ -414,7 +446,7 @@
     @pl.loop(0, 8)
     def _(j):
         when_at(j, backward_events)
-        backward_clients(2 * j, 2, cg_ref, wo_ref, q_ref, kv_ref, pt_ref, mc_ref, dkv_ref, att_ref)
+        backward_clients(2 * j, 2, cg_ref, wo_ref, q_ref, kv_ref, pt_ref, mc_ref, dkv_ref, datt_ref, ds_ref)
 
     go_ref = ns_ref.at[pl.ds(0, D)]
     done = [
@@ -455,19 +487,19 @@
         step_kernel,
         out_shape=(
             sds((TOK, D), BF), sds((D, D), BF), sds((D, 2 * TOK), BF), sds((D, D), BF),
-            sds((3, width, D), BF), sds((3, width, D), BF),
+            *[sds((width, D), BF)] * 6,
         ),
         in_specs=[pl.BlockSpec(memory_space=pltpu.SMEM)] + [vmem] * 4 + [anyspace] * 6,
-        out_specs=[vmem] + [anyspace] * 5,
+        out_specs=[vmem] + [anyspace] * 9,
         scratch_shapes=[
             pltpu.VMEM((D, D), BF), pltpu.VMEM((D, 2 * TOK), BF), pltpu.VMEM((D, D), BF), pltpu.VMEM((3, units, D), BF),
             blocks(16), blocks(16), pltpu.VMEM((D, 16 * TOK), BF), pltpu.VMEM((D, 16 * TOK), BF),
-            blocks(16), pltpu.VMEM((16, TOK, 2 * TOK), BF), pltpu.VMEM((16, PAIRS, 2 * TOK, TOK), BF),
-            pltpu.VMEM((2 * TOK, D), BF),
+            pltpu.VMEM((16, PAIRS, TOK, TOK), BF), pltpu.VMEM((16, TOK, 2 * TOK), BF), pltpu.VMEM((16, 2 * TOK, D), BF),
+            pltpu.VMEM((2, PAIRS, TOK, TOK), BF), pltpu.VMEM((2, 2 * TOK, D), BF),
             blocks(8), pltpu.VMEM((3, units, D), BF), pltpu.VMEM((8 * TOK, D), BF), pltpu.VMEM((3, units, 8 * TOK), BF),
             pltpu.VMEM((TOK, D), F32), pltpu.VMEM((16, 8, D), BF), pltpu.VMEM((15, 8, D), BF), pltpu.VMEM((8, D), BF),
             pltpu.VMEM((16, 8, D), BF), blocks(16), blocks(7), pltpu.VMEM((16, TOK, 2 * TOK), BF),
-            sem((6,)), sem((18,)), sem((18,)), sem((17,)), sem((17,)), sem((3,)), sem((3,)), sem((15,)), sem((15,)),
+            sem((6,)), sem((16,)), sem((16,)), sem((17,)), sem((17,)), sem((3,)), sem((3,)), sem((15,)), sem((15,)),
             sem((15,)), sem((15,)), sem((17,)), sem((17,)), sem((15,)), sem((15,)), sem((7,)), sem((7,)),
             sem((3,)), sem((3,)), sem((3,)),
         ],
@@ -479,19 +511,19 @@
 def on_device(
     client_input, client_gain, w_query, w_keyval, w_out, server_gain, w_gate, w_up, w_down, out_grad, valid
 ):
-    server_out, grad_q, grad_kv, grad_o, own, got = step_call(
+    server_out, grad_q, grad_kv, grad_o, *shards = step_call(
         valid, client_input[0, 0], out_grad[0, 0], client_gain, server_gain, w_query[0], w_keyval[0], w_out[0],
         w_gate[0].T, w_up[0].T, w_down[0],
     )
-    joined = (own.astype(F32) + got.astype(F32)).astype(BF)
+    gate, up, down = [(own.astype(F32) + got.astype(F32)).astype(BF) for own, got in zip(shards[:3], shards[3:])]
     return (
         server_out[None, None],
         grad_q[None],
         grad_kv[None],
         grad_o[None],
-        joined[0].T[None],
-        joined[1].T[None],
-        joined[2][None],
+        gate.T[None],
+        up.T[None],
+        down[None],
     )
 
 

time: 130 us -> 108 us (0.83)
  Pallas kernels: 121 us -> 99.1 us
  other arithmetic: 2.32 us -> 3.82 us
  local copies, waits for them, and re-layouts: 5.43 us -> 4.01 us
    pallas_call x1, Pallas kernels: 121 us -> 99.1 us  [step_call(): pl.pallas_call(step_kernel, out_shape=(sds((TOK, D), BF), sds((D, D), BF)...]
    broadcast_in_dim x0 -> x2, other arithmetic: none -> 3.82 us  [the longest x1 2.88 us: on_device(): gate.T[None]]
    convert_element_type x1 -> x0, other arithmetic: 2.32 us -> none  [on_device(): joined = (own.astype(F32) + got.astype(F32)).astype(BF)]
    unnamed x12 -> x16, local copies, waits for them, and re-layouts: 4.23 us -> 4.01 us
where the time goes in v3:
time: 108 us
  Pallas kernels  99.1 us (92%)
  local copies, waits for them, and re-layouts  4.01 us (4%)
  other arithmetic  3.82 us (4%)
  between operations  1.33 us (1%)
    pallas_call x1, Pallas kernels, step_call(): pl.pallas_call(step_kernel, out_shape=(sds((TOK, D), BF), sds((D, D), BF)...  99.1 us
    unnamed x16, local copies, waits for them, and re-layouts  4.01 us
    broadcast_in_dim x1, other arithmetic, on_device(): gate.T[None]  2.88 us

profile of v3, /device:TPU:1, one launch (start us, length us, event | category | flops | bytes accessed | tf_op | source)
XLA Modules:
  0.0 108.3 jit_solution(14367268014333186571)
XLA Ops:
  1.3 99.1 %split_step.1 = (bf16[128,896]{1,0:T(8,128)(2,1)}, bf16[896,896]{1,0:T(8,128)(2,1)}, bf16[896,256]{1,0:T(8,128)(2,1)}, bf16[896,896]{1,0:T(8,128)(2,1)}, bf16[30...) custom-call(s32[1,1]{1,0:T(1,128)S(6)} %copy.22.valid_ref, ...), custom_call_target="tpu_custom_call" | custom-call | tf_op jit(solution)/shard_map/split_step/pallas_call | solution.py:486
  100.4 0.0 copy-start.2
  100.4 0.0 copy-start.3
  100.5 0.0 copy-start.5
  100.5 2.9 %fusion = (bf16[1,896,304]{1,2,0:T(8,128)(2,1)}, bf16[1,896,304]{1,2,0:T(8,128)(2,1)}) fusion(bf16[304,896]{1,0:T(8,128)(2,1)} %get-tuple-element.22, bf16[304,896]{1,0:T(8,128)(2,1)} %get-tuple-element.21, bf16[304,896]{1,0:T(8,128)(2,1)} %get-tuple-element.24, bf16[304,896]{1,0:T(8,128)(2,1)} %get-tuple-element.23), kind=kLoop, calls=%fused_computation.3 | loop fusion | flops 2179072 | bytes 3268608 | tf_op jit(solution)/shard_map/broadcast_in_dim | solution.py:524
  103.3 0.0 copy-start.1
  103.3 0.0 copy-done.2
  103.4 0.0 copy-done.3
  103.4 0.9 fusion.2
  104.3 0.0 copy-done.5
  104.3 0.7 copy.23
  105.0 0.0 copy-done.1
  105.0 0.0 copy-start.4
  105.0 0.0 copy-start
  105.0 1.2 %copy.24 = bf16[1,896,896]{2,1,0:T(8,128)(2,1)} copy(bf16[1,896,896]{2,1,0:T(8,128)(2,1)S(1)} %bitcast.29) | data formatting | bytes 3211264
  106.1 0.1 copy-done.4
  106.3 0.8 copy.25
  107.1 0.1 copy-done
  107.1 1.2 %copy.26 = bf16[1,896,896]{2,1,0:T(8,128)(2,1)} copy(bf16[1,896,896]{2,1,0:T(8,128)(2,1)S(1)} %bitcast.28) | data formatting | bytes 3211264
Async XLA Ops:
  100.4 2.9 %copy-start.2 = (bf16[304,896]{1,0:T(8,128)(2,1)S(1)}, bf16[304,896]{1,0:T(8,128)(2,1)}, u32[]{:S(2)}) copy-start(bf16[304,896]{1,0:T(8,128)(2,1)} %get-tuple-element.25) | copy-start | bytes 1634308
  100.4 2.9 %copy-start.3 = (bf16[304,896]{1,0:T(8,128)(2,1)S(1)}, bf16[304,896]{1,0:T(8,128)(2,1)}, u32[]{:S(2)}) copy-start(bf16[304,896]{1,0:T(8,128)(2,1)} %get-tuple-element.26) | copy-start | bytes 1634308
  100.5 3.8 %copy-start.5 = (bf16[128,896]{1,0:T(8,128)(2,1)S(1)}, bf16[128,896]{1,0:T(8,128)(2,1)}, u32[]{:S(2)}) copy-start(bf16[128,896]{1,0:T(8,128)(2,1)} %get-tuple-element.17) | copy-start | bytes 688132
  103.3 1.6 %copy-start.1 = (bf16[896,896]{1,0:T(8,128)(2,1)S(1)}, bf16[896,896]{1,0:T(8,128)(2,1)}, u32[]{:S(2)}) copy-start(bf16[896,896]{1,0:T(8,128)(2,1)} %get-tuple-element.18) | copy-start | bytes 4816900
  105.0 1.3 %copy-start.4 = (bf16[896,256]{1,0:T(8,128)(2,1)S(1)}, bf16[896,256]{1,0:T(8,128)(2,1)}, u32[]{:S(2)}) copy-start(bf16[896,256]{1,0:T(8,128)(2,1)} %get-tuple-element.19) | copy-start | bytes 1376260
  105.0 2.1 %copy-start = (bf16[896,896]{1,0:T(8,128)(2,1)S(1)}, bf16[896,896]{1,0:T(8,128)(2,1)}, u32[]{:S(2)}) copy-start(bf16[896,896]{1,0:T(8,128)(2,1)} %get-tuple-element.20) | copy-start | bytes 4816900

commit v4 on v3

--- a/solution.py
+++ b/solution.py
@@ -69,8 +69,8 @@
 GROUPS = ((0, 3), (3, 4), (4, 7))
 
 
-def head_rows(both):
-    wide = both.astype(F32)
+def head_rows(both, scale=1.0):
+    wide = both.astype(F32) * scale
     turned = pltpu.roll(wide, HEAD_DIM, 1)
     low = lax.broadcasted_iota(jnp.int32, wide.shape, 1) < HEAD_DIM
     zero = jnp.zeros_like(wide)
@@ -117,8 +117,8 @@
         for head in range(2):
             span = MEETS[place][head]
             for n in range(count):
-                keys = head_rows(kv[n * TOK : (n + 1) * TOK, :TOK])
-                scores = mm(keys[place][head], stack(q_ref, slot + n, span), NT) * SCALE
+                keys = head_rows(kv[n * TOK : (n + 1) * TOK, :TOK], SCALE)
+                scores = mm(keys[place][head], stack(q_ref, slot + n, span), NT)
                 for p in range(*span):
                     s = jnp.where(seen, scores[:, lanes((p - span[0], p - span[0] + 1))], -1e30)
                     e = jnp.exp(s - jnp.max(s, axis=0, keepdims=True))
@@ -150,11 +150,11 @@
                 for p in range(*span):
                     wide = pt_ref[slot + n, keys_at, lanes((p, p + 1))].astype(F32)
                     both = d_probs[:, lanes((p - span[0], p - span[0] + 1))] * wide
-                    ds = (both - wide * jnp.sum(both, axis=0, keepdims=True)) * SCALE
+                    ds = both - wide * jnp.sum(both, axis=0, keepdims=True)
                     ds_ref[n, keys_at, lanes((p, p + 1))] = ds.astype(BF)
     low = lax.broadcasted_iota(jnp.int32, (TOK, TOK), 1) < HEAD_DIM
     for n in range(count):
-        keys = head_columns(kv_ref[slot + n, :, :TOK])
+        keys = head_columns((kv_ref[slot + n, :, :TOK].astype(F32) * SCALE).astype(BF))
         for span, part in zip(GROUPS, keys):
             out = mm(part, ds_ref[n, :, lanes(span)]).astype(BF)
             for p in range(*span):
@@ -167,18 +167,104 @@
             ]
             first = total[0][0] + pltpu.roll(total[1][0], HEAD_DIM, 1)
             second = total[1][1] + pltpu.roll(total[0][1], HEAD_DIM, 1)
-            dkv_ref[slot + n, :, lanes((at, at + 1))] = jnp.where(low, first, second).astype(BF)
-
-
-def last_products(left_ref, pairs):
-    step = D // 2
+            dkv_ref[slot + n, :, lanes((at, at + 1))] = (jnp.where(low, first, second) * (SCALE if at == 0 else 1.0)).astype(BF)
+
+
+def last_products(left_ref, rows, pairs):
+    for right_ref, out_ref in pairs:
+        right = right_ref[...].reshape(16 * TOK, right_ref.shape[-1])
+        out_ref[rows, :] = (mm(left_ref[rows, :], right) * (1.0 / 16)).astype(BF)
+
+
+def finish_kernel(
+    served_hbm, nt_hbm, at_hbm, dq_hbm, dkv_hbm, cg_hbm, own_g, own_u, own_d, got_g, got_u, got_d,
+    out_hbm, gq_hbm, gkv_hbm, go_hbm, gate_hbm, up_hbm, down_hbm,
+    served_ref, nt_ref, at_ref, dq_ref, dkv_ref, cg_ref, own_ref, got_ref, gq_ref, gkv_ref, go_ref, load, store,
+):
+    half = D // 2
+    top, low = pl.ds(0, half), pl.ds(half, half)
+    moves = [
+        (cg_hbm, cg_ref), (at_hbm.at[top], at_ref.at[top]), (at_hbm.at[low], at_ref.at[low]),
+        (own_g, own_ref.at[0]), (own_u, own_ref.at[1]), (own_d, own_ref.at[2]),
+        (got_g, got_ref.at[0]), (got_u, got_ref.at[1]), (got_d, got_ref.at[2]),
+        (served_hbm, served_ref), (dq_hbm, dq_ref), (dkv_hbm, dkv_ref),
+        (nt_hbm.at[top], nt_ref.at[top]), (nt_hbm.at[low], nt_ref.at[low]),
+    ]
+    loads = [pltpu.make_async_copy(s, d, load.at[k]) for k, (s, d) in enumerate(moves)]
+    for copy in loads:
+        copy.start()
+    stores = [
+        (go_ref, go_hbm), (own_ref.at[0], gate_hbm), (own_ref.at[1], up_hbm), (own_ref.at[2], down_hbm),
+        (served_ref, out_hbm), (gq_ref.at[top], gq_hbm.at[top]), (gkv_ref.at[top], gkv_hbm.at[top]),
+        (gq_ref.at[low], gq_hbm.at[low]), (gkv_ref.at[low], gkv_hbm.at[low]),
+    ]
+    stores = [pltpu.make_async_copy(s, d, store.at[k]) for k, (s, d) in enumerate(stores)]
+
+    def await_loads(*which):
+        for k in which:
+            loads[k].wait()
 
     @pl.loop(0, 2)
     def _(t):
-        rows = pl.ds(pl.multiple_of(t * step, step), step)
-        for right_ref, out_ref in pairs:
-            right = right_ref[...].reshape(16 * TOK, right_ref.shape[-1])
-            out_ref[rows, :] = (mm(left_ref[rows, :], right) * (1.0 / 16)).astype(BF)
+        @pl.when(t == 0)
+        def _():
+            await_loads(0, 1)
+
+        @pl.when(t == 1)
+        def _():
+            await_loads(2)
+
+        last_products(at_ref, pl.ds(pl.multiple_of(t * half, 64), half), [(cg_ref, go_ref)])
+
+    await_loads(*range(3, 10))
+    stores[4].start()
+    for k in range(3):
+        own_ref[k] = (own_ref[k].astype(F32) + got_ref[k].astype(F32)).astype(BF)
+    stores[0].start()
+
+    @pl.loop(0, 2)
+    def _(t):
+        @pl.when(t == 0)
+        def _():
+            await_loads(10, 11, 12)
+            for copy in stores[1:4]:
+                copy.start()
+
+        @pl.when(t == 1)
+        def _():
+            await_loads(13)
+            for copy in stores[5:7]:
+                copy.start()
+
+        last_products(nt_ref, pl.ds(pl.multiple_of(t * half, 64), half), [(dq_ref, gq_ref), (dkv_ref, gkv_ref)])
+
+    for copy in stores[7:]:
+        copy.start()
+    for copy in stores:
+        copy.wait()
+
+
+def finish_call(*args):
+    anyspace = pl.BlockSpec(memory_space=pl.ANY)
+    sds = jax.ShapeDtypeStruct
+    width = args[6].shape[0]
+    blocks = lambda n: pltpu.VMEM((n, TOK, D), BF)
+    return pl.pallas_call(
+        finish_kernel,
+        out_shape=(
+            sds((TOK, D), BF), sds((D, D), BF), sds((D, 2 * TOK), BF), sds((D, D), BF), *[sds((width, D), BF)] * 3,
+        ),
+        in_specs=[anyspace] * 12,
+        out_specs=[anyspace] * 7,
+        scratch_shapes=[
+            pltpu.VMEM((TOK, D), BF), pltpu.VMEM((D, 16 * TOK), BF), pltpu.VMEM((D, 16 * TOK), BF), blocks(16),
+            pltpu.VMEM((16, TOK, 2 * TOK), BF), blocks(16), pltpu.VMEM((3, width, D), BF), pltpu.VMEM((3, width, D), BF),
+            pltpu.VMEM((D, D), BF), pltpu.VMEM((D, 2 * TOK), BF), pltpu.VMEM((D, D), BF),
+            pltpu.SemaphoreType.DMA((14,)), pltpu.SemaphoreType.DMA((9,)),
+        ],
+        compiler_params=pltpu.CompilerParams(vmem_limit_bytes=60 * 1024 * 2**10),
+        name="finish",
+    )(*args)
 
 
 def server_rows(j, mc_ref, sgain, ws_ref, served_ref, ns_ref, act_ref, sum_ref):
@@ -219,11 +305,11 @@
 
 def step_kernel(
     valid_ref, x_ref, cot_ref, gain_ref, sgain_ref, wq_hbm, wkv_hbm, wo_hbm, wg_hbm, wu_hbm, wd_hbm,
-    out_ref, gq_hbm, gkv_hbm, go_hbm, own_g, own_u, own_d, got_g, got_u, got_d,
+    out_ref, nt_hbm, at_hbm, dq_hbm, dkv_hbm, cg_hbm, own_g, own_u, own_d, got_g, got_u, got_d,
     wq_ref, wkv_ref, wo_ref, ws_ref, xs_ref, mc_ref, nt_ref, at_ref, q_ref, kv_ref, pt_ref, datt_ref, ds_ref,
     served_ref, gr_ref, ns_ref, act_ref, sum_ref, ls_ref, part_ref, mine_ref, slices_ref, cg_ref, back_ref, dkv_ref,
     load, send_m, recv_m, send_x, recv_x, send_w, recv_w, send_r, recv_r, send_a, recv_a,
-    send_z, recv_z, send_c, recv_c, send_s, recv_s, send_g, recv_g, keep,
+    send_z, recv_z, send_c, recv_c, send_s, recv_s, send_g, recv_g, keep, leave_sem,
 ):
     pos = places()
     m, c = pos["m"], pos["c"]
@@ -299,7 +385,7 @@
     ]
     keeps = [pltpu.make_async_copy(gr_ref.at[k, near], own, keep.at[k]) for k, own in enumerate((own_g, own_u, own_d))]
 
-    for copy in [in_ring[1, 0, 0], in_ring[1, 0, 1]] + cot[:2] + [in_across, cot[2]] + swap:
+    for copy in [in_ring[1, 0, 0], in_ring[1, 0, 1]] + cot[:2] + [in_across, cot[2]]:
         copy.start()
     sum_ref[...] = mc_ref[8].astype(F32)
     gain, sgain = gain_ref[...], sgain_ref[...]
@@ -308,7 +394,7 @@
     saved = (nt_ref, at_ref, q_ref, kv_ref, pt_ref)
     xf = forward_clients(0, 1, xs_ref, gain, wq_ref, wkv_ref, *saved)
     mc_ref[0] = (xf + mm(at_ref[:, :TOK], wo_ref[...], TN)).astype(BF)
-    for copy in cut[:3]:
+    for copy in cut[:3] + swap:
         copy.start()
 
     def from_neighbours(copies):
@@ -372,7 +458,7 @@
         for d in range(15):
             spread[d].wait_recv()
         cg_ref[0] = slices_ref[...].astype(F32).reshape(TOK, D).astype(BF)
-        for copy in [cg_across, cg_ring[1, 0, 0], cg_ring[1, 0, 1]] + serve + trade + keeps:
+        for copy in [cg_across, cg_ring[1, 0, 0], cg_ring[1, 0, 1]] + trade + keeps:
             copy.start()
 
     def when_at(i, events):
@@ -382,20 +468,25 @@
                 for act in todo:
                     act()
 
+    def go(copies):
+        for copy in copies:
+            copy.start()
+
     before_rows = {
         0: [lambda: from_neighbours(cot), lambda: inputs(1, 0), first_inputs],
         1: [server_weights, lambda: from_across(cot), lambda: from_neighbours(cut)],
         2: [lambda: from_across(cut), lambda: from_far(cot)],
-        4: [lambda: inputs(3, 0), lambda: arrived(5, 6)],
-        5: [lambda: arrived(7)],
-        6: [lambda: inputs(3, 1), own_group],
-        7: [lambda: inputs(4, 0), lambda: inputs(4, 1)],
+        3: [lambda: arrived(5, 6)],
+        4: [lambda: arrived(7)],
+        5: [gradients, reduce],
+        6: [lambda: inputs(3, 1)],
+        7: [lambda: inputs(4, 0), lambda: inputs(4, 1), own_group],
     }
     before_pair = {
         1: [lambda: inputs(2, 0)],
         2: [lambda: inputs(1, 1), lambda: from_far(cut)],
-        4: [lambda: inputs(2, 1)],
-        5: [share, gradients, reduce],
+        3: [lambda: go(serve[:3])],
+        4: [share, lambda: inputs(3, 0), lambda: inputs(2, 1)],
     }
     order = sum(pair << (3 * k) for k, pair in enumerate((1, 3, 0, 2, 5, 4, 6, 7)))
 
@@ -403,9 +494,9 @@
     def _(k):
         when_at(k, before_rows)
 
-        @pl.when((k % 3 != 0) & (k < 6))
+        @pl.when((k >= 1) & (k <= 4))
         def _():
-            server_rows(k - 1 - k // 4, mc_ref, sgain, ws_ref, served_ref, ns_ref, act_ref, sum_ref)
+            server_rows(k - 1, mc_ref, sgain, ws_ref, served_ref, ns_ref, act_ref, sum_ref)
 
         when_at(k, before_pair)
         pair = jnp.right_shift(order, 3 * k) % 8
@@ -432,15 +523,27 @@
 
     for copy in cot + cut:
         copy.wait_send()
+    whole = pltpu.make_async_copy(cg_ref, cg_hbm, load.at[0])
+    strip = D // 8
+    leave = [
+        [
+            pltpu.make_async_copy(s.at[pl.ds(size * j, size)], d.at[pl.ds(size * j, size)], leave_sem.at[4 * j + k])
+            for k, (s, d, size) in enumerate(
+                [(nt_ref, nt_hbm, strip), (at_ref, at_hbm, strip), (mc_ref, dq_hbm, 2), (dkv_ref, dkv_hbm, 2)]
+            )
+        ]
+        for j in range(8)
+    ]
+
     backward_events = {
         0: [first_grads, lambda: grads(1, 0), lambda: handed(1)],
-        1: [lambda: grads(1, 1), lambda: handed(2, 3)],
-        2: [lambda: grads(2, 0), lambda: handed(4, 5)],
-        3: [lambda: grads(2, 1), lambda: handed(6, 7)],
-        4: [lambda: grads(3, 0), lambda: handed(8, 9)],
-        5: [lambda: grads(3, 1), lambda: handed(10, 11)],
-        6: [lambda: grads(4, 0), lambda: grads(4, 1), lambda: handed(12, 13)],
-        7: [lambda: handed(14, 15)],
+        1: [lambda: grads(1, 1), lambda: handed(2, 3), lambda: go(serve[3:] + leave[0])],
+        2: [lambda: grads(2, 0), lambda: handed(4, 5), lambda: go(leave[1])],
+        3: [lambda: grads(2, 1), lambda: handed(6, 7), lambda: go(leave[2])],
+        4: [lambda: grads(3, 0), lambda: handed(8, 9), lambda: go(leave[3])],
+        5: [lambda: grads(3, 1), lambda: handed(10, 11), lambda: go(leave[4])],
+        6: [lambda: grads(4, 0), lambda: grads(4, 1), lambda: handed(12, 13), lambda: go(leave[5] + leave[7][:2])],
+        7: [lambda: handed(14, 15), lambda: go(leave[6] + [whole])],
     }
 
     @pl.loop(0, 8)
@@ -448,17 +551,8 @@
         when_at(j, backward_events)
         backward_clients(2 * j, 2, cg_ref, wo_ref, q_ref, kv_ref, pt_ref, mc_ref, dkv_ref, datt_ref, ds_ref)
 
-    go_ref = ns_ref.at[pl.ds(0, D)]
-    done = [
-        pltpu.make_async_copy(s, d, load.at[k])
-        for k, (s, d) in enumerate([(go_ref, go_hbm), (wq_ref, gq_hbm), (wkv_ref, gkv_hbm)])
-    ]
-    last_products(at_ref, [(cg_ref, go_ref)])
-    done[0].start()
-    last_products(nt_ref, [(mc_ref, wq_ref), (dkv_ref, wkv_ref)])
-    done[1].start()
-    done[2].start()
-
+    for copy in leave[7][2:]:
+        copy.start()
     for copy in serve:
         copy.wait_recv()
     out = sum_ref[...] + served_ref[0].astype(F32)
@@ -467,7 +561,7 @@
     out_ref[...] = out.astype(BF)
     for copy in trade:
         copy.wait_recv()
-    for copy in keeps + done:
+    for copy in keeps + [whole] + sum(leave, []):
         copy.wait()
     for copy in [in_across, cg_across] + list(in_ring.values()) + list(cg_ring.values()) + list(over.values()):
         copy.wait_send()
@@ -486,11 +580,11 @@
     return pl.pallas_call(
         step_kernel,
         out_shape=(
-            sds((TOK, D), BF), sds((D, D), BF), sds((D, 2 * TOK), BF), sds((D, D), BF),
-            *[sds((width, D), BF)] * 6,
+            sds((TOK, D), BF), sds((D, 16 * TOK), BF), sds((D, 16 * TOK), BF), sds((16, TOK, D), BF),
+            sds((16, TOK, 2 * TOK), BF), sds((16, TOK, D), BF), *[sds((width, D), BF)] * 6,
         ),
         in_specs=[pl.BlockSpec(memory_space=pltpu.SMEM)] + [vmem] * 4 + [anyspace] * 6,
-        out_specs=[vmem] + [anyspace] * 9,
+        out_specs=[vmem] + [anyspace] * 11,
         scratch_shapes=[
             pltpu.VMEM((D, D), BF), pltpu.VMEM((D, 2 * TOK), BF), pltpu.VMEM((D, D), BF), pltpu.VMEM((3, units, D), BF),
             blocks(16), blocks(16), pltpu.VMEM((D, 16 * TOK), BF), pltpu.VMEM((D, 16 * TOK), BF),
@@ -501,7 +595,7 @@
             pltpu.VMEM((16, 8, D), BF), blocks(16), blocks(7), pltpu.VMEM((16, TOK, 2 * TOK), BF),
             sem((6,)), sem((16,)), sem((16,)), sem((17,)), sem((17,)), sem((3,)), sem((3,)), sem((15,)), sem((15,)),
             sem((15,)), sem((15,)), sem((17,)), sem((17,)), sem((15,)), sem((15,)), sem((7,)), sem((7,)),
-            sem((3,)), sem((3,)), sem((3,)),
+            sem((3,)), sem((3,)), sem((3,)), sem((32,)),
         ],
         compiler_params=pltpu.CompilerParams(collective_id=0, has_side_effects=True, vmem_limit_bytes=60 * 1024 * 2**10),
         name="split_step",
@@ -511,11 +605,11 @@
 def on_device(
     client_input, client_gain, w_query, w_keyval, w_out, server_gain, w_gate, w_up, w_down, out_grad, valid
 ):
-    server_out, grad_q, grad_kv, grad_o, *shards = step_call(
+    parts = step_call(
         valid, client_input[0, 0], out_grad[0, 0], client_gain, server_gain, w_query[0], w_keyval[0], w_out[0],
         w_gate[0].T, w_up[0].T, w_down[0],
     )
-    gate, up, down = [(own.astype(F32) + got.astype(F32)).astype(BF) for own, got in zip(shards[:3], shards[3:])]
+    server_out, grad_q, grad_kv, grad_o, gate, up, down = finish_call(*parts)
     return (
         server_out[None, None],
         grad_q[None],

time: 108 us -> 106 us (0.981)
  Pallas kernels: 99.1 us -> 104 us
  local copies, waits for them, and re-layouts: 4.01 us -> 0 us
  other arithmetic: 3.82 us -> 0 us
    pallas_call x1 -> x2, Pallas kernels: 99.1 us -> 104 us  [the longest x1 90.9 us: step_call(): pl.pallas_call(step_kernel, out_shape=(sds((TOK, D), BF), sds((D, 16 * TO...]
    unnamed x16 -> x0, local copies, waits for them, and re-layouts: 4.01 us -> none
    broadcast_in_dim x2 -> x0, other arithmetic: 3.82 us -> none  [the longest x1 2.88 us: on_device(): gate.T[None]]
where the time goes in v4:
time: 106 us
  Pallas kernels  104 us (98%)
  between operations  1.29 us (1%)
    pallas_call x1, Pallas kernels, step_call(): pl.pallas_call(step_kernel, out_shape=(sds((TOK, D), BF), sds((D, 16 * TO...  90.9 us
    pallas_call x1, Pallas kernels, finish_call(): pl.pallas_call(finish_kernel, out_shape=(sds((TOK, D), BF), sds((D, D), B...  13.4 us

profile of v4, /device:TPU:1, one launch (start us, length us, event | category | flops | bytes accessed | tf_op | source)
XLA Modules:
  0.0 105.5 jit_solution(4379668885228464983)
XLA Ops:
  1.3 90.9 %split_step.1 = (bf16[128,896]{1,0:T(8,128)(2,1)}, bf16[896,2048]{1,0:T(8,128)(2,1)}, bf16[896,2048]{1,0:T(8,128)(2,1)}, bf16[16,128,896]{2,1,0:T(8,128)(2,1)}, ...) custom-call(s32[1,1]{1,0:T(1,128)S(6)} %copy.18.valid_ref, ...), custom_call_target="tpu_custom_call" | custom-call | tf_op jit(solution)/shard_map/split_step/pallas_call | solution.py:580
  92.1 13.4 %finish.1 = (bf16[128,896]{1,0:T(8,128)(2,1)}, bf16[896,896]{1,0:T(8,128)(2,1)}, bf16[896,256]{1,0:T(8,128)(2,1)}, bf16[896,896]{1,0:T(8,128)(2,1)}, bf16[304,89...) custom-call(bf16[128,896]{1,0:T(8,128)(2,1)} %get-tuple-element.26.served_hbm, ...), custom_call_target="tpu_custom_call" | custom-call | tf_op jit(solution)/shard_map/finish/pallas_call | solution.py:252
